TPU v7x, 512 devices: a whole 4x4x16 slice. The times are simulated.
512 devices in a mesh: pb: 8 (over y_lo, x), ka: 64 (over z, y_hi, core).
Axes of the slice: x: 4, y: 4 (y_hi: 2, y_lo: 2; y = y_hi * 2 + y_lo), z: 16, core: 2. Of those that a mesh axis runs over, the one named last changes fastest.
Arguments:
- coupling: bfloat16 [20480, 8, 2048], P('ka', 'pb'), may hold values from -0.0048828125 to 0.0048828125
- eigvec: float32 [64, 2048], P('ka'), may hold values from -0.75 to 0.75
- energies: float32 [64, 32], P('ka'), may hold values from -1 to 1
- k_coords: int32 [3, 64], replicated, may hold values from 0 to 63
- r_coords: int32 [3, 20480], P(None, 'ka'), may hold values from -12 to 12
- degeneracy: int32 [20480], P('ka'), may hold values from 1 to 8
- kq_index: int32 [64, 96], P('ka', 'pb'), may hold values from 0 to 63
- omega: float32 [96, 8], P('pb'), may hold values from 0.05 to 0.5
- phonon_modes: float32 [96, 8, 8], P('pb'), may hold values from -2 to 2
Outputs:
- sigma: float32 [64, 32], P('ka', 'pb')
All inputs are finite; a program needn't handle non-finite values.
Results may differ from a plain program's by a relative error of at most 0.0013.
Values may be sent and summed in bfloat16 or wider, within the bound.
A program may use at most 64 MiB of HBM per device.

v0:
```python
import math

import jax
import jax.numpy as jnp
from jax import lax
from jax.sharding import PartitionSpec as P

KGRID = 64


THERMAL = 0.1
SMEARING = 0.05
HIGHEST = lax.Precision.HIGHEST


def in_blocks(x, dim, count):
    before, after = (x.shape[:dim], x.shape[dim + 1 :])
    return jnp.moveaxis(x.reshape(*before, count, -1, *after), dim, 0)


def sent_and_summed(x, axis, dim):
    count = lax.axis_size(axis)
    tiles = lax.all_to_all(in_blocks(x, dim, count), axis, 0, 0, tiled=True)
    return jnp.sum(tiles, axis=0)


def in_order(tiles, dim):
    shape = list(tiles.shape[1:])
    shape[dim] *= tiles.shape[0]
    return jnp.moveaxis(tiles, 0, dim).reshape(shape)


def copy_for_each(x, axis):
    count = lax.axis_size(axis)
    return lax.all_to_all(jnp.broadcast_to(x[None], (count, *x.shape)), axis, 0, 0, tiled=True)


def gather_directly(x, axis, dim):
    return in_order(copy_for_each(x, axis), dim)


def in_one_piece(arrays, axis, dim, along):
    ends, at = ([], 0)
    for a in arrays[:-1]:
        at += a.shape[along]
        ends.append(at)
    both = jnp.concatenate(arrays, axis=along)
    return tuple(jnp.split(gather_directly(both, axis, dim), ends, axis=along))


def phases(k_coords, r_coords, degeneracy):
    turns = (
        k_coords[0][:, None] * r_coords[0][None, :]
        + k_coords[1][:, None] * r_coords[1][None, :]
        + k_coords[2][:, None] * r_coords[2][None, :]
    ) % KGRID
    angle = turns.astype(jnp.float32) * (2.0 * math.pi / KGRID)
    inverse = 1.0 / degeneracy.astype(jnp.float32)
    cosine = (jnp.cos(angle) * inverse[None, :]).astype(jnp.bfloat16)
    sine = (jnp.sin(angle) * inverse[None, :]).astype(jnp.bfloat16)
    return (cosine, sine)


def combine_parts(cosine_sum, sine_sum, modes, square):
    cosine_rows = cosine_sum.reshape(cosine_sum.shape[0], modes, 2, square)
    sine_rows = sine_sum.reshape(sine_sum.shape[0], modes, 2, square)
    real_part = cosine_rows[:, :, 0] - sine_rows[:, :, 1]
    imag_part = cosine_rows[:, :, 1] + sine_rows[:, :, 0]
    return jnp.stack([real_part, imag_part], axis=2).reshape(
        cosine_sum.shape[0], modes * 2 * square
    )


def lorentz(spacing):
    return SMEARING / (math.pi * (spacing * spacing + SMEARING * SMEARING))


def self_energy(wannier, vector, energy, kq_vectors, kq_energies, omega, phonon):
    bands = energy.shape[0]
    modes = wannier.shape[0]
    matrix = wannier.astype(jnp.float32).reshape(modes, 2, bands, bands)
    rotate = vector.reshape(2, bands, bands)
    fold_real = jnp.einsum("vac,cn->van", matrix[:, 0], rotate[0], precision=HIGHEST) - jnp.einsum(
        "vac,cn->van", matrix[:, 1], rotate[1], precision=HIGHEST
    )
    fold_imag = jnp.einsum("vac,cn->van", matrix[:, 0], rotate[1], precision=HIGHEST) + jnp.einsum(
        "vac,cn->van", matrix[:, 1], rotate[0], precision=HIGHEST
    )
    mixed_real = jnp.einsum("qwv,wan->qvan", phonon, fold_real, precision=HIGHEST)
    mixed_imag = jnp.einsum("qwv,wan->qvan", phonon, fold_imag, precision=HIGHEST)
    target = kq_vectors.reshape(-1, 2, bands, bands)
    final_real = jnp.einsum(
        "qam,qvan->qmvn", target[:, 0], mixed_real, precision=HIGHEST
    ) + jnp.einsum("qam,qvan->qmvn", target[:, 1], mixed_imag, precision=HIGHEST)
    final_imag = jnp.einsum(
        "qam,qvan->qmvn", target[:, 0], mixed_imag, precision=HIGHEST
    ) - jnp.einsum("qam,qvan->qmvn", target[:, 1], mixed_real, precision=HIGHEST)
    strength = final_real * final_real + final_imag * final_imag
    fermi = 1.0 / (1.0 + jnp.exp(kq_energies / THERMAL))
    bose = 1.0 / jnp.expm1(omega / THERMAL)
    spacing = energy[None, None, None, :] - kq_energies[:, :, None, None]
    absorb = lorentz(spacing + omega[:, None, :, None])
    emit = lorentz(spacing - omega[:, None, :, None])
    bose_wide = bose[:, None, :, None]
    fermi_wide = fermi[:, :, None, None]
    occupy = (bose_wide + fermi_wide) * absorb + (bose_wide + 1.0 - fermi_wide) * emit
    return jnp.sum(strength * occupy, axis=(0, 1, 2))


def fourier_terms(k_coords, r_coords, degeneracy, slab, modes, square, count):
    cosine, sine = phases(k_coords, r_coords, degeneracy)
    stacked = jnp.dot(
        jnp.concatenate([cosine, sine], axis=0), slab, preferred_element_type=jnp.float32
    )
    return combine_parts(stacked[:count], stacked[count:], modes, square)


def shards(
    coupling, eigvec, energies, k_coords, r_coords, degeneracy, kq_index, omega, phonon_modes
):
    bands = energies.shape[1]
    points = eigvec.shape[0]
    local_modes = coupling.shape[1]
    slab = coupling.reshape(coupling.shape[0], -1)
    partial_value = sent_and_summed(
        fourier_terms(
            k_coords,
            r_coords,
            degeneracy,
            slab,
            local_modes,
            bands * bands,
            points * lax.axis_size("ka"),
        ),
        "ka",
        0,
    )
    own_wannier = partial_value.astype(jnp.bfloat16).reshape(points, local_modes, 2 * bands * bands)
    wannier = gather_directly(own_wannier, "pb", 1)
    pairs = kq_index.reshape(-1)
    pieces = in_one_piece((eigvec, energies), "ka", 0, 1)
    labels = jnp.arange(pieces[0].shape[0], dtype=jnp.int32)
    hits = (pairs[:, None] == labels[None, :]).astype(jnp.float32)
    vectors_sum = jnp.dot(hits, pieces[0], precision=HIGHEST, preferred_element_type=jnp.float32)
    energy_sum = jnp.dot(hits, pieces[1], precision=HIGHEST, preferred_element_type=jnp.float32)
    kq_vectors = vectors_sum
    kq_energies = energy_sum
    queries = kq_index.shape[1]
    kq_vectors = kq_vectors.reshape(points, queries, eigvec.shape[1])
    kq_energies = kq_energies.reshape(points, queries, bands)

    def per_point(items):
        wannier_row, vector, energy, kq_rows, kq_levels = items
        return self_energy(wannier_row, vector, energy, kq_rows, kq_levels, omega, phonon_modes)

    sigma = lax.map(per_point, (wannier, eigvec, energies, kq_vectors, kq_energies))
    sigma = sigma / (queries * lax.axis_size("pb"))
    return sent_and_summed(sigma, "pb", 1)


def solution(mesh):
    in_specs = (
        P("ka", "pb", None),
        P("ka", None),
        P("ka", None),
        P(),
        P(None, "ka"),
        P("ka"),
        P("ka", "pb"),
        P("pb", None),
        P("pb", None, None),
    )
    out_specs = P("ka", "pb")
    return jax.shard_map(shards, mesh=mesh, in_specs=in_specs, out_specs=out_specs, check_vma=False)
```

profile of v0, /device:TPU:1, one launch (start us, length us, event | category | flops | bytes accessed | tf_op | source)
XLA Modules:
  0.0 139.1 jit_solution(14746882562933434113)
XLA Ops:
  0.0 0.0 copy-start
  0.0 0.8 slice_bitcast_fusion.14
  0.8 0.7 convert_divide_fusion
  1.5 0.8 slice_reduce_fusion.4
  2.3 0.5 multiply_convert_fusion.1
  2.9 0.0 copy-done
  2.9 0.4 fusion
  3.3 0.1 fusion.32
  3.4 0.4 reshape.105
  3.8 0.4 reshape.106
  4.3 0.5 slice_subtract_fusion
  4.8 0.5 pad_maximum_fusion
  5.3 0.0 copy-start.4
  5.3 0.0 copy-start.9
  5.3 0.8 reshape_reshape.3
  6.2 0.0 copy-start.5
  6.2 53.5 %all_to_all.20 = f32[64,1,2048]{2,1,0:T(1,128)S(1)} all-to-all(f32[64,1,2048]{2,1,0:T(1,128)S(1)} %reshape_reshape.3), channel_id=1, replica_groups=mesh['pb'=8,'ka'=64] {'ka'}, dimensions={0} | all-to-all | bytes 1048576 | tf_op jit(solution)/shard_map/all_to_all | solution.py:23
  59.7 0.4 reduce_sum.30
  60.1 0.5 broadcast.131
  60.6 0.8 reduce.19
  61.4 0.6 reshape.135
  62.1 4.1 %all-to-all-start.2 = ((bf16[8,2,1024]{2,1,0:T(2,128)(2,1)}), bf16[8,2,1024]{2,1,0:T(2,128)(2,1)S(1)}, u32[]{:S(2)}, u32[]{:S(2)}) async-start(bf16[8,2,1024]{2,1,0:T(2,128)(2,1)} %reshape.135), calls=%async_computation.2 | async-start | bytes 65536 | tf_op jit(solution)/shard_map/all_to_all | solution.py:35
  66.2 0.0 copy-done.4
  66.2 0.0 copy-done.9
  66.2 0.0 copy-start.3
  66.3 5.0 %all-to-all-done.2 = bf16[8,2,1024]{2,1,0:T(2,128)(2,1)S(1)} async-done(((bf16[8,2,1024]{2,1,0:T(2,128)(2,1)}), bf16[8,2,1024]{2,1,0:T(2,128)(2,1)S(1)}, u32[]{:S(2)}, u32[]{:S(2)}) %all-to-all-start.2) | async-done | bytes 32800 | tf_op jit(solution)/shard_map/all_to_all | solution.py:35
  71.3 1.1 broadcast_in_dim.14
  72.4 7.2 %all-to-all-start = ((f32[64,1,2080]{2,1,0:T(1,128)}), f32[64,1,2080]{2,1,0:T(1,128)}, u32[]{:S(2)}, u32[]{:S(2)}) async-start(f32[64,1,2080]{2,1,0:T(1,128)} %broadcast_in_dim.14), calls=%async_computation | async-start | bytes 1114112 | tf_op jit(solution)/shard_map/all_to_all | solution.py:35
  79.6 0.0 copy-done.5
  79.6 0.7 copy.45
  80.3 0.1 copy.44
  80.4 0.1 copy.46
  80.5 0.1 reshape.108
  80.6 0.1 reshape.109
  80.7 0.2 reduce.6
  80.9 0.1 reshape.107
  81.0 0.2 fusion.21
  81.2 0.2 fusion.9
  81.4 0.2 fusion.22
  81.6 0.2 fusion.10
  81.8 0.0 copy-done.3
  81.8 3.2 %convolution_bitcast_fusion.1 = f32[12,8,32,32]{3,0,1,2:T(8,128)} fusion(f32[8,32,32,1]{2,1,0,3:T(8,128)S(1)} %fusion.10, f32[12,8,8]{0,2,1:T(8,128)S(1)} %copy-done.3), kind=kOutput, calls=%fused_computation.1 | convolution fusion | flops 9437184 | bytes 429056 | tf_op jit(solution)/shard_map/while/body/eval_jaxpr/qwv,wan->qvan/dot_general | solution.py:89
  85.1 1.9 %convolution_bitcast_fusion = f32[12,8,32,32]{3,0,1,2:T(8,128)S(1)} fusion(f32[8,32,32,1]{2,1,0,3:T(8,128)S(1)} %fusion.9, f32[12,8,8]{0,2,1:T(8,128)S(1)} %copy-done.3), kind=kOutput, calls=%fused_computation | convolution fusion | flops 9437184 | bytes 429056 | tf_op jit(solution)/shard_map/while/body/eval_jaxpr/qwv,wan->qvan/dot_general | solution.py:90
  86.9 27.9 %all-to-all-done = f32[64,1,2080]{2,1,0:T(1,128)} async-done(((f32[64,1,2080]{2,1,0:T(1,128)}), f32[64,1,2080]{2,1,0:T(1,128)}, u32[]{:S(2)}, u32[]{:S(2)}) %all-to-all-start) | async-done | bytes 532512 | tf_op jit(solution)/shard_map/all_to_all | solution.py:35
  114.8 1.1 copy.82
  115.9 0.0 copy-done.11
  115.9 0.8 add_divide_fusion
  116.7 1.0 fusion.11
  117.7 0.9 reshape.103
  118.6 3.5 %fusion.2 = f32[12,32,8,32]{3,1,2,0:T(8,128)S(1)} fusion(f32[12,8,32,32]{3,0,1,2:T(8,128)S(1)} %convolution_bitcast_fusion, f32[12,2,32,32]{3,2,1,0:T(8,128)} %reshape.103), kind=kOutput, calls=%fused_computation.5 | convolution fusion | flops 37748736 | bytes 983040 | tf_op jit(solution)/shard_map/while/body/eval_jaxpr/qam,qvan->qmvn/dot_general | solution.py:95
  122.1 0.0 copy-done.2
  122.1 0.0 copy-start.1
  122.1 2.5 %fusion.4 = f32[12,32,8,32]{3,1,2,0:T(8,128)S(1)} fusion(f32[12,8,32,32]{3,0,1,2:T(8,128)S(1)} %convolution_bitcast_fusion, f32[12,2,32,32]{3,2,1,0:T(8,128)S(1)} %copy-done.2), kind=kOutput, calls=%fused_computation.7 | convolution fusion | flops 37748736 | bytes 2686976 | tf_op jit(solution)/shard_map/while/body/eval_jaxpr/qam,qvan->qmvn/dot_general | solution.py:94
  124.6 0.0 copy-done.1
  124.6 0.0 copy-start.6
  124.6 0.0 copy-start.10
  124.7 2.5 %fusion.7 = f32[12,32,8,32]{3,1,2,0:T(8,128)S(1)} fusion(f32[12,8,32,32]{3,0,1,2:T(8,128)S(1)} %copy-done.1, f32[12,2,32,32]{3,2,1,0:T(8,128)S(1)} %copy-done.2), kind=kOutput, calls=%fused_computation.10 | convolution fusion | flops 37748736 | bytes 2686976 | tf_op jit(solution)/shard_map/while/body/eval_jaxpr/qam,qvan->qmvn/dot_general | solution.py:92
  127.2 0.1 broadcast_subtract_fusion
  127.3 0.0 copy-done.8
  127.3 0.1 broadcast_add_fusion
  127.4 3.7 %multiply_reduce_fusion = f32[32]{0:T(128)S(1)} fusion(f32[12,32,8,32]{3,1,2,0:T(8,128)S(1)} %fusion.2, f32[12,32,8,32]{3,1,2,0:T(8,128)S(1)} %fusion.7, f32[12,32,8,32]{3,1,2,0:T(8,128)S(1)} %fusion.4, f32[12,8,32,32]{3,0,1,2:T(8,128)S(1)} %copy-done.1, f32[12,32,8]{1,2,0:T(8,128)S(1)} %get-tuple-element.44, f32[12,8]{1,0:T(8,128)S(1)} %copy-done.7, ...), kind=kOutput, calls=%fused_computation.2 | convolution fusion | flops 39714784 | bytes 7315584 | tf_op jit(solution)/shard_map/while/body/eval_jaxpr/qam,qvan->qmvn/dot_general | solution.py:97
  131.1 0.1 div.48
  131.1 7.4 %all_to_all.21 = f32[8,1,4]{2,1,0:T(1,128)S(1)} all-to-all(f32[8,1,4]{2,1,0:T(1,128)S(1)} %bitcast.68), channel_id=1, replica_groups=mesh['pb'=8,'ka'=64] {'pb'}, dimensions={0} | all-to-all | bytes 256 | tf_op jit(solution)/shard_map/all_to_all | solution.py:23
  138.5 0.5 reduce_sum.32
  (13 shorter events, 0.2 us)
Async XLA Ops:
  0.0 2.9 %copy-start = (bf16[320,1,2048]{2,0,1:T(8,128)(2,1)S(1)}, bf16[320,1,2048]{2,0,1:T(8,128)(2,1)}, u32[]{:S(2)}) copy-start(bf16[320,1,2048]{2,0,1:T(8,128)(2,1)} %param.9) | copy-start | bytes 3932164
  5.3 60.9 %copy-start.4 = (f32[1,2048]{1,0:T(1,128)S(1)}, f32[1,2048]{1,0:T(1,128)}, u32[]{:S(2)}) copy-start(f32[1,2048]{1,0:T(1,128)} %param.10) | copy-start | bytes 24580
  5.3 60.9 %copy-start.9 = (f32[1,32]{1,0:T(1,128)S(1)}, f32[1,32]{1,0:T(1,128)}, u32[]{:S(2)}) copy-start(f32[1,32]{1,0:T(1,128)} %param.11) | copy-start | bytes 388
  6.2 73.5 %copy-start.5 = (f32[12,8]{0,1:T(8,128)S(1)}, f32[12,8]{0,1:T(8,128)}, u32[]{:S(2)}) copy-start(f32[12,8]{0,1:T(8,128)} %param.16) | copy-start | bytes 1156
  62.1 9.2 %all-to-all-start.2 = ((bf16[8,2,1024]{2,1,0:T(2,128)(2,1)}), bf16[8,2,1024]{2,1,0:T(2,128)(2,1)S(1)}, u32[]{:S(2)}, u32[]{:S(2)}) async-start(bf16[8,2,1024]{2,1,0:T(2,128)(2,1)} %reshape.135), calls=%async_computation.2 | async-start | bytes 65536 | tf_op jit(solution)/shard_map/all_to_all | solution.py:35
  66.2 15.6 %copy-start.3 = (f32[12,8,8]{0,2,1:T(8,128)S(1)}, f32[12,8,8]{0,2,1:T(8,128)}, u32[]{:S(2)}) copy-start(f32[12,8,8]{0,2,1:T(8,128)} %param.17) | copy-start | bytes 9220
  72.4 42.4 %all-to-all-start = ((f32[64,1,2080]{2,1,0:T(1,128)}), f32[64,1,2080]{2,1,0:T(1,128)}, u32[]{:S(2)}, u32[]{:S(2)}) async-start(f32[64,1,2080]{2,1,0:T(1,128)} %broadcast_in_dim.14), calls=%async_computation | async-start | bytes 1114112 | tf_op jit(solution)/shard_map/all_to_all | solution.py:35
  85.1 30.8 %copy-start.11 = (s32[1,12]{1,0:T(1,128)S(1)}, s32[1,12]{1,0:T(1,128)}, u32[]{:S(2)}) copy-start(s32[1,12]{1,0:T(1,128)} %param.15) | copy-start | bytes 148
  118.6 3.5 %copy-start.2 = (f32[12,2,32,32]{3,2,1,0:T(8,128)S(1)}, f32[12,2,32,32]{3,2,1,0:T(8,128)}, u32[]{:S(2)}) copy-start(f32[12,2,32,32]{3,2,1,0:T(8,128)} %reshape.103) | copy-start | bytes 294916
  122.1 2.5 %copy-start.1 = (f32[12,8,32,32]{3,0,1,2:T(8,128)S(1)}, f32[12,8,32,32]{3,0,1,2:T(8,128)}, u32[]{:S(2)}) copy-start(f32[12,8,32,32]{3,0,1,2:T(8,128)} %convolution_bitcast_fusion.1) | copy-start | bytes 1179652
  124.6 2.5 %copy-start.6 = (f32[12,32]{1,0:T(8,128)S(1)}, f32[12,32]{1,0:T(8,128)}, u32[]{:S(2)}) copy-start(f32[12,32]{1,0:T(8,128)} %get-tuple-element.51) | copy-start | bytes 4612
  124.6 2.5 %copy-start.10 = (f32[1,32]{1,0:T(1,128)S(1)}, f32[1,32]{1,0:T(1,128)}, u32[]{:S(2)}) copy-start(f32[1,32]{1,0:T(1,128)} %param.11) | copy-start | bytes 388
  124.6 2.7 %copy-start.8 = (f32[12,32]{1,0:T(8,128)S(1)}, f32[12,32]{1,0:T(8,128)}, u32[]{:S(2)}) copy-start(f32[12,32]{1,0:T(8,128)} %get-tuple-element.50) | copy-start | bytes 4612
  124.6 2.7 %copy-start.7 = (f32[12,8]{1,0:T(8,128)S(1)}, f32[12,8]{1,0:T(8,128)}, u32[]{:S(2)}) copy-start(f32[12,8]{1,0:T(8,128)} %copy.45) | copy-start | bytes 1156
where the time goes:
time: 140 us; the launch traced here: 139 us
  blocking collectives  60.9 us (44%)
  waiting for transfers between devices  32.9 us (24%)
  matrix products  20.2 us (14%)
  starting transfers between devices  11.3 us (8%)
  local copies, waits for them, and re-layouts  9.01 us (6%)
  other arithmetic  4.37 us (3%)
    all_to_all x2, blocking collectives, sent_and_summed(): tiles = lax.all_to_all(in_blocks(x, dim, count), axis, 0, 0, tiled=True)  60.9 us
    all_to_all x2, waiting for transfers between devices, copy_for_each(): lax.all_to_all(jnp.broadcast_to(x[None], (count, *x.shape)), axis, 0, 0,...  32.9 us
    all_to_all x2, starting transfers between devices, copy_for_each(): lax.all_to_all(jnp.broadcast_to(x[None], (count, *x.shape)), axis, 0, 0,...  11.3 us
    dot_general x1, matrix products, self_energy(): jnp.einsum('qam,qvan->qmvn', target[:, 1], mixed_real, precision=HIGHEST)  3.65 us
    dot_general x1, matrix products, self_energy(): jnp.einsum('qam,qvan->qmvn', target[:, 0], mixed_imag, precision=HIGHEST)  3.48 us
    dot_general x1, matrix products, self_energy(): jnp.einsum('qwv,wan->qvan', phonon, fold_real, precision=HIGHEST)  3.22 us
  transfers between devices with their start and end apart: 2, of which 2 were waited for; matrix products, arithmetic and copies ran while one was open for 5% of the time, Pallas kernels for 0%

commit v1 on v0

v1 whole, which is shorter than its diff:
```python
import functools
import math

import jax
import jax.numpy as jnp
from jax import lax
from jax.experimental import pallas as pl
from jax.experimental.pallas import tpu as pltpu
from jax.sharding import PartitionSpec as P

THERMAL = 0.1
SMEARING = 0.05
NB = 32
LANES = 128
SLOTS = 16
V_EARLY = 16
MESH = pl.DeviceIdType.MESH
BF = jnp.bfloat16
F32 = jnp.float32


def iota(shape, dim):
    return lax.broadcasted_iota(jnp.int32, shape, dim)


def spin(x, shift):
    shift = shift % LANES
    return x if shift == 0 else pltpu.roll(x, shift, 1)


def pieces(x, count):
    out = []
    for _ in range(count):
        part = x.astype(BF)
        out.append(part)
        x = x - part.astype(F32)
    return out


def body(
    np_, ka, ql,
    coup, vec, ener, kc, rc, deg, kq, om, ph,
    out,
    xbuf, sums, sendc, recvc, sendz, recvz, vsend, vgot, esend, egot,
    flat, posend, pogot, kqsend, kqgot, kqs, spread, phx, fold, fsend, fgot,
    turned, vq, occ, eq,
    xsem, csem, zsend, zrecv, vs_sem, vr_sem, es_sem, er_sem, wsem,
    ps_sem, pr_sem, ks_sem, kr_sem, ksm, fs_sem, fr_sem,
):
    ni = ka // 2
    nz = ni // 2
    nb = NB // np_
    rows = 2 * nb
    queries = ql * np_
    width = queries * NB
    tiles = width // LANES
    rl = coup.shape[0]
    me = lax.axis_index("ka")
    mp = lax.axis_index("pb")
    mc = lax.rem(me, 2)
    mi = me // 2
    mz = mi // 2
    my = lax.rem(mi, 2)
    other = {"ka": mi * 2 + (1 - mc)}

    def chip(o):
        s = o // 2
        dz = nz // 2 + ((s + 1) // 2) * (1 - 2 * lax.rem(s, 2))
        z = lax.rem(mz + dz + nz, nz)
        y = lax.rem(my + 1 - lax.rem(o, 2), 2)
        return z * 2 + y

    def mate(o):
        return lax.rem(mp + 1 + o, np_)

    def each(count, f):
        def step(o, carry):
            f(o)
            return carry
        lax.fori_loop(0, count, step, 0)

    barrier = pltpu.get_barrier_semaphore()
    each(ni - 1, lambda o: pl.semaphore_signal(
        barrier, inc=1, device_id={"ka": chip(o) * 2 + mc}, device_id_type=MESH))
    pl.semaphore_signal(barrier, inc=1, device_id=other, device_id_type=MESH)
    each(np_ - 1, lambda o: pl.semaphore_signal(
        barrier, inc=1, device_id={"pb": mate(o)}, device_id_type=MESH))

    load = pltpu.make_async_copy(coup, xbuf, xsem)
    load.start()

    kpad = jnp.concatenate(
        [kc[...].astype(F32), jnp.zeros((5, ka), F32)], axis=0)
    if ka < LANES:
        kpad = jnp.concatenate([kpad, jnp.zeros((8, LANES - ka), F32)], axis=1)
    kcol = jnp.transpose(jnp.concatenate([kpad, jnp.zeros((LANES - 8, LANES), F32)], axis=0))[:ka]
    rrow = rc[...].astype(F32)
    turns = (kcol[:, 0:1] * rrow[0:1, :] + kcol[:, 1:2] * rrow[1:2, :]) + kcol[:, 2:3] * rrow[2:3, :]
    x = turns - 64.0 * jnp.floor(turns * (1.0 / 64.0))
    quad = jnp.floor((x + 8.0) * (1.0 / 16.0))
    a = (x - 16.0 * quad) * (2.0 * math.pi / 64.0)
    a2 = a * a
    sin_a = a + a * a2 * (-1.0 / 6 + a2 * (1.0 / 120 + a2 * (-1.0 / 5040 + a2 * (1.0 / 362880))))
    cos_a = 1.0 + a2 * (-0.5 + a2 * (1.0 / 24 + a2 * (-1.0 / 720 + a2 * (1.0 / 40320))))
    odd = (quad == 1.0) | (quad == 3.0)
    cosine = jnp.where(odd, sin_a, cos_a)
    sine = jnp.where(odd, cos_a, sin_a)
    cosine = jnp.where((quad == 1.0) | (quad == 2.0), -cosine, cosine)
    sine = jnp.where((quad == 2.0) | (quad == 3.0), -sine, sine)
    inverse = 1.0 / deg[...].astype(F32)
    both = jnp.concatenate([cosine * inverse, sine * inverse], axis=0).astype(BF)

    load.wait()
    cut = min(256, rl)

    def product(at):
        total = jnp.dot(both[:, :cut], xbuf[:cut, at : at + 256], preferred_element_type=F32)
        if rl > cut:
            total += jnp.dot(both[:, cut:], xbuf[cut:, at : at + 256], preferred_element_type=F32)
        return total

    for j in range(4):
        re, im = product(256 * j), product(1024 + 256 * j)
        real = re[:ka] - im[ka:]
        imag = im[:ka] + re[ka:]
        for h in range(2):
            t = 2 * j + h
            sums[t * ka : (t + 1) * ka, :] = real[:, h * LANES : (h + 1) * LANES]
            sums[(8 + t) * ka : (9 + t) * ka, :] = imag[:, h * LANES : (h + 1) * LANES]

    def of_point(k):
        return sums[pl.ds(k, 16, stride=ka), :]

    def to_partner(i):
        sendc[i] = of_point(2 * i + (1 - mc)).astype(BF)
    each(ni, to_partner)

    lane8 = iota((8, LANES), 1)
    v = vec[...]
    vsend[...] = v.astype(BF)
    flat[...] = jnp.zeros_like(flat)
    flat[0:1, 0:NB] = ener[...]
    erow = flat[0:8, :]
    erow = (erow + spin(erow, 32)) + (spin(erow, 64) + spin(erow, 96))
    esend[...] = erow[0:1, :]
    flat[0:1, 0:NB] = jnp.zeros((1, NB), F32)
    flat[0 : np_ * np_, 0:ql] = ph[...]
    flat[64 : 64 + np_, 0:ql] = om[...]
    posend[...] = jnp.transpose(flat[...])[:SLOTS]
    kqsend[...] = jnp.zeros_like(kqsend)
    kqsend[0:1, 0:ql] = kq[...]

    pl.semaphore_wait(barrier, ni + np_ - 1)

    def copy(src, dst, s, r, to):
        return pltpu.make_async_remote_copy(
            src_ref=src, dst_ref=dst, send_sem=s, recv_sem=r, device_id=to, device_id_type=MESH)

    swap = copy(sendc, recvc, csem.at[0], csem.at[1], other)
    swap.start()

    def po_copy(o, to):
        return copy(posend, pogot.at[mp], ps_sem.at[o], pr_sem.at[mp], {"pb": to})

    def kq_copy(o, to):
        return copy(kqsend, kqgot.at[mp], ks_sem.at[o], kr_sem.at[mp], {"pb": to})

    def small(o):
        po_copy(o, mate(o)).start()
        kq_copy(o, mate(o)).start()
    each(np_ - 1, small)
    pogot[mp] = posend[...]
    kqgot[mp] = kqsend[...]

    def e_copy(o, i):
        return copy(esend, egot.at[mc, mi], es_sem.at[o], er_sem.at[mi], {"ka": i * 2 + mc})

    def v_copy(o, i):
        return copy(vsend, vgot.at[mc, mi], vs_sem.at[o], vr_sem.at[mi], {"ka": i * 2 + mc})

    def z_copy(o, i):
        return copy(sendz.at[i], recvz.at[mi], zsend.at[o], zrecv.at[mi], {"ka": i * 2 + mc})

    early = min(V_EARLY, ni - 1)

    def first(o):
        v_copy(o, chip(o)).start()
    each(early, first)
    each(ni - 1, lambda o: e_copy(o, chip(o)).start())
    vgot[mc, mi] = vsend[...]
    egot[mc, mi] = esend[...]

    swap.wait_recv()

    def add_and_send(o):
        i = chip(o)
        sendz[i] = (of_point(2 * i + mc) + recvc[i].astype(F32)).astype(BF)
        z_copy(o, i).start()
    each(ni - 1, add_and_send)
    own = of_point(me) + recvc[mi].astype(F32)

    def late(o):
        v_copy(o + early, chip(o + early)).start()
    each(ni - 1 - early, late)

    for blk, (s0, c0, s1, c1) in enumerate(
        [(1, 0, 1, 1), (-1, 1, 1, 0), (1, 1, -1, 0), (1, 0, 1, 1)]
    ):
        for low in range(4):
            left = s0 * spin(v[8 * c0 : 8 * c0 + 8], -32 * low)
            right = s1 * spin(v[8 * c1 : 8 * c1 + 8], 32 - 32 * low)
            val = jnp.where(lane8 < 32, left, jnp.where(lane8 < 64, right, 0.0))
            flat[pl.ds(32 * blk + low, 8, stride=4), :] = val
    table = jnp.transpose(flat[...])[:64]
    r_at, c_at = iota((64, 64), 0), iota((64, 64), 1)
    pick = (((r_at // nb) % 2) * NB + (r_at // rows) * nb + r_at % nb == c_at).astype(F32).astype(BF)
    for h, part in enumerate(pieces(table, 2)):
        fold[:, h * LANES : (h + 1) * LANES] = jnp.dot(
            pick, part, preferred_element_type=F32).astype(BF)

    q_at = iota((LANES, width), 1) // NB
    spread[...] = ((q_at // ql) * SLOTS + q_at % ql == iota((LANES, width), 0)).astype(F32).astype(BF)

    def small_wait(o):
        src = mate(o)
        po_in = copy(posend, pogot.at[src], ps_sem.at[o], pr_sem.at[src], {"pb": src})
        po_in.wait_recv()
        kq_in = copy(kqsend, kqgot.at[src], ks_sem.at[o], kr_sem.at[src], {"pb": src})
        kq_in.wait_recv()
    each(np_ - 1, small_wait)
    to_scalar = pltpu.make_async_copy(kqgot, kqs, ksm)
    to_scalar.start()
    got = pogot[...].reshape(np_ * SLOTS, LANES)
    if np_ * SLOTS < LANES:
        got = jnp.concatenate([got, jnp.zeros((LANES - np_ * SLOTS, LANES), F32)], axis=0)
    three = pieces(jnp.transpose(got)[:72], 3)
    three = [jnp.concatenate([p.astype(F32), jnp.zeros((8, LANES), F32)], axis=0).astype(BF) for p in three]
    for j in range(width // 256 if width % 256 == 0 else 0):
        at = slice(256 * j, 256 * j + 256)
        total = jnp.dot(three[0], spread[:, at], preferred_element_type=F32)
        total += jnp.dot(three[1], spread[:, at], preferred_element_type=F32)
        total += jnp.dot(three[2], spread[:, at], preferred_element_type=F32)
        phx[:, at] = total
    to_scalar.wait()

    def z_wait(o, total):
        i = chip(o)
        copy(sendz.at[i], recvz.at[i], zsend.at[o], zrecv.at[i], {"ka": i * 2 + mc}).wait_recv()
        return total + recvz[i].astype(F32)
    wann = lax.fori_loop(0, ni - 1, z_wait, own).astype(BF).astype(F32)
    blocks = []
    for low in range(4):
        for part in range(2):
            at = 64 * part
            w0 = spin(wann[0:8], at - 32 * low)
            w1 = spin(wann[8:16], at + 32 - 32 * low)
            blocks.append(jnp.where(
                (lane8 >= at) & (lane8 < at + 32), w0,
                jnp.where((lane8 >= at + 32) & (lane8 < at + 64), w1, 0.0)))
    right = jnp.concatenate(blocks + [jnp.zeros((64, LANES), F32)], axis=0).astype(BF)
    right = jnp.concatenate([right, right], axis=1)
    folded = lax.dot_general(
        fold[...], right, (((1,), (1,)), ((), ())), preferred_element_type=F32)
    for p in range(np_):
        fsend[p] = folded[p * rows : (p + 1) * rows]

    def f_copy(o, to):
        return copy(fsend.at[to], fgot.at[mp], fs_sem.at[o], fr_sem.at[mp], {"pb": to})
    each(np_ - 1, lambda o: f_copy(o, mate(o)).start())
    fgot[mp] = fsend[mp]

    def v_wait(o):
        i = chip(o)
        copy(vsend, vgot.at[mc, i], vs_sem.at[o], vr_sem.at[i], {"ka": i * 2 + mc}).wait_recv()
        copy(esend, egot.at[mc, i], es_sem.at[o], er_sem.at[i], {"ka": i * 2 + mc}).wait_recv()
    each(ni - 1, v_wait)
    give_v = copy(vgot.at[mc], vgot.at[mc], wsem.at[0], wsem.at[1], other)
    give_e = copy(egot.at[mc], egot.at[mc], wsem.at[2], wsem.at[3], other)
    give_v.start()
    give_e.start()

    def rolled(c):
        def step(i):
            val = vgot[c, i].astype(F32)
            turned[0, c, i] = val
            for s in range(1, 4):
                turned[s, c, i] = spin(val, 32 * s)
        each(ni, step)
    rolled(mc)
    copy(vgot.at[1 - mc], vgot.at[1 - mc], wsem.at[0], wsem.at[1], other).wait_recv()
    copy(egot.at[1 - mc], egot.at[1 - mc], wsem.at[2], wsem.at[3], other).wait_recv()
    rolled(1 - mc)

    lane16 = iota((16, LANES), 1) // NB
    lane1 = iota((1, LANES), 1) // NB
    row_e = iota((rows, LANES), 0) % nb + mp * nb
    e_col = jnp.sum(
        jnp.where(iota((rows, LANES), 1) == row_e, esend[...], 0.0), axis=1, keepdims=True)

    def by_group(mask, vals):
        return jnp.where(mask == 0, vals[0], jnp.where(
            mask == 1, vals[1], jnp.where(mask == 2, vals[2], vals[3])))

    def tables(t):
        at = pl.ds(pl.multiple_of(t * LANES, LANES), LANES)
        where = []
        for g in range(4):
            q = 4 * t + g
            point = kqs[q // ql, 0, lax.rem(q, ql)]
            where.append((lax.rem(point, 2), point // 2))
        for low in range(4):
            vq[16 * low : 16 * low + 16, at] = by_group(
                lane16, [turned[(g - low) % 4, where[g][0], where[g][1]] for g in range(4)]).astype(BF)
        e_there = by_group(lane1, [egot[where[g][0], where[g][1]] for g in range(4)])
        fermi = 1.0 / (1.0 + jnp.exp(e_there * (1.0 / THERMAL)))
        gap = e_col - e_there
        omega = phx[64:72, at]
        bose = 1.0 / (jnp.exp(omega * (1.0 / THERMAL)) - 1.0)
        for m in range(np_):
            w, b = omega[m : m + 1], bose[m : m + 1]
            up, down = gap + w, gap - w
            scale = SMEARING / (math.pi * queries)
            value = (b + fermi) * (scale / (up * up + SMEARING * SMEARING))
            value += (b + 1.0 - fermi) * (scale / (down * down + SMEARING * SMEARING))
            occ[m, :, at] = value
    each(tiles, tables)

    def f_wait(o):
        src = mate(o)
        copy(fsend.at[src], fgot.at[src], fs_sem.at[o], fr_sem.at[src], {"pb": src}).wait_recv()
    each(np_ - 1, f_wait)
    left = fgot[...].reshape(np_ * rows, LANES)[:, :64].astype(BF)

    def finish(t, total):
        at = pl.ds(pl.multiple_of(t * 256, 256), 256)
        h = jnp.dot(left, vq[:, at], preferred_element_type=F32)
        for m in range(np_):
            g = phx[m : m + 1, at] * h[0:rows]
            for w in range(1, np_):
                g += phx[w * np_ + m : w * np_ + m + 1, at] * h[w * rows : (w + 1) * rows]
            total += (g * g) * occ[m, :, at]
        return total
    total = lax.fori_loop(0, width // 256, finish, jnp.zeros((rows, 256), F32))
    summed = jnp.sum(total, axis=1, keepdims=True)
    out[...] = jnp.sum(
        jnp.where(iota((rows, LANES), 1) == iota((rows, LANES), 0) % nb, summed, 0.0),
        axis=0, keepdims=True)[:, :nb]

    swap.wait_send()
    give_v.wait_send()
    give_e.wait_send()

    def drain(o):
        i = chip(o)
        z_copy(o, i).wait_send()
        v_copy(o, i).wait_send()
        e_copy(o, i).wait_send()
    each(ni - 1, drain)

    def drain_small(o):
        po_copy(o, mate(o)).wait_send()
        kq_copy(o, mate(o)).wait_send()
        f_copy(o, mate(o)).wait_send()
    each(np_ - 1, drain_small)


def shards(mesh, coupling, eigvec, energies, k_coords, r_coords, degeneracy, kq_index, omega, phonon_modes):
    np_, ka = mesh.shape["pb"], mesh.shape["ka"]
    rl = coupling.shape[0]
    ql = omega.shape[0]
    ni = ka // 2
    nb = NB // np_
    rows = 2 * nb
    width = ql * np_ * NB
    vm = pl.BlockSpec(memory_space=pltpu.VMEM)
    hbm = pl.BlockSpec(memory_space=pl.ANY)
    V = pltpu.VMEM
    sem = pltpu.SemaphoreType.DMA
    return pl.pallas_call(
        functools.partial(body, np_, ka, ql),
        out_shape=jax.ShapeDtypeStruct((1, nb), F32),
        in_specs=[hbm] + [vm] * 8,
        out_specs=vm,
        scratch_shapes=[
            V((rl, 2048), BF),
            V((16 * ka, LANES), F32),
            V((ni, 16, LANES), BF),
            V((ni, 16, LANES), BF),
            V((ni, 16, LANES), BF),
            V((ni, 16, LANES), BF),
            V((16, LANES), BF),
            V((2, ni, 16, LANES), BF),
            V((1, LANES), F32),
            V((2, ni, 1, LANES), F32),
            V((LANES, LANES), F32),
            V((SLOTS, LANES), F32),
            V((np_, SLOTS, LANES), F32),
            V((1, LANES), jnp.int32),
            V((np_, 1, LANES), jnp.int32),
            pltpu.SMEM((np_, 1, LANES), jnp.int32),
            V((LANES, width), BF),
            V((80, width), F32),
            V((64, 256), BF),
            V((np_, rows, LANES), F32),
            V((np_, rows, LANES), F32),
            V((4, 2, ni, 16, LANES), F32),
            V((64, width), BF),
            V((np_, rows, width), F32),
            V((1, LANES), F32),
            sem, sem((2,)), sem((ni,)), sem((ni,)), sem((ni,)), sem((ni,)), sem((ni,)), sem((ni,)), sem((4,)),
            sem((np_,)), sem((np_,)), sem((np_,)), sem((np_,)), sem, sem((np_,)), sem((np_,)),
        ],
        compiler_params=pltpu.CompilerParams(collective_id=0, has_side_effects=True),
        name="self_energy",
    )(
        coupling.reshape(rl, 2048),
        eigvec.reshape(16, LANES),
        energies,
        k_coords,
        r_coords,
        degeneracy.reshape(1, rl),
        kq_index,
        omega.T,
        jnp.transpose(phonon_modes, (1, 2, 0)).reshape(np_ * np_, ql),
    )


def solution(mesh):
    in_specs = (
        P("ka", "pb", None),
        P("ka", None),
        P("ka", None),
        P(),
        P(None, "ka"),
        P("ka"),
        P("ka", "pb"),
        P("pb", None),
        P("pb", None, None),
    )
    return jax.shard_map(
        functools.partial(shards, mesh), mesh=mesh, in_specs=in_specs,
        out_specs=P("ka", "pb"), check_vma=False)
```

time: 140 us -> 47.3 us (0.34)
  blocking collectives: 60.9 us -> 0 us
  Pallas kernels: 0 us -> 44.7 us
  waiting for transfers between devices: 32.9 us -> 0 us
  matrix products: 20.2 us -> 0 us
  starting transfers between devices: 11.3 us -> 0 us
  local copies, waits for them, and re-layouts: 9.01 us -> 2.38 us
  other arithmetic: 4.37 us -> 0 us
    all_to_all x2 -> x0, blocking collectives: 60.9 us -> none  [sent_and_summed(): tiles = lax.all_to_all(in_blocks(x, dim, count), axis, 0, 0, tiled=True)]
    pallas_call x0 -> x1, Pallas kernels: none -> 44.7 us  [shards(): pl.pallas_call(functools.partial(body, np_, ka, ql), out_shape=jax.ShapeD...]
    all_to_all x2 -> x0, waiting for transfers between devices: 32.9 us -> none  [copy_for_each(): lax.all_to_all(jnp.broadcast_to(x[None], (count, *x.shape)), axis, 0, 0,...]
    dot_general x13 -> x0, matrix products: 20.2 us -> none  [the longest x1 3.65 us: self_energy(): jnp.einsum('qam,qvan->qmvn', target[:, 1], mixed_real, precision=HIGHEST)]
    all_to_all x2 -> x0, starting transfers between devices: 11.3 us -> none  [copy_for_each(): lax.all_to_all(jnp.broadcast_to(x[None], (count, *x.shape)), axis, 0, 0,...]
    broadcast_in_dim x3 -> x0, local copies, waits for them, and re-layouts: 1.66 us -> none  [copy_for_each(): jnp.broadcast_to(x[None], (count, *x.shape))]
  transfers between devices with their start and end apart: 2 -> 0, of which waited for: 2 -> 0; matrix products, arithmetic and copies ran while one was open for 5% -> 0% of each run, Pallas kernels for 0% -> 0%
where the time goes in v1:
time: 47.3 us; the launch traced here: 47.1 us
  Pallas kernels  44.7 us (95%)
  local copies, waits for them, and re-layouts  2.38 us (5%)
    pallas_call x1, Pallas kernels, shards(): pl.pallas_call(functools.partial(body, np_, ka, ql), out_shape=jax.ShapeD...  44.7 us
    reshape x1, local copies, waits for them, and re-layouts, shards(): degeneracy.reshape(1, rl)  1.27 us
    unnamed x1, local copies, waits for them, and re-layouts  1.11 us

profile of v1, /device:TPU:1, one launch (start us, length us, event | category | flops | bytes accessed | tf_op | source)
XLA Modules:
  0.0 47.1 jit_solution(8915558375774628112)
XLA Ops:
  0.0 1.3 %reshape.14.deg = s32[1,320]{1,0:T(1,128)} reshape(s32[320]{0:T(512)} %param.14) | data formatting | bytes 2560 | tf_op jit(solution)/shard_map/reshape | solution.py:421
  1.3 44.7 %self_energy.1 = f32[1,4]{1,0:T(1,128)} custom-call(bf16[320,2048]{1,0:T(8,128)(2,1)} %bitcast.6, f32[16,128]{1,0:T(8,128)} %bitcast.8, f32[1,32]{1,0:T(1,128)} %ener.1, s32[3,64]{1,0:T(4,128)} %kc.1, s32[3,320]{1,0:T(4,128)} %rc.1, s32[1,320]{1,0:T(1,128)} %reshape.14.deg, s32[1,12]{1,0:T(1,128)} %kq.1, f32[8,12]{1,0:T(8,128)} %bitcast.9, f32[64,12]{1,0:T(8,128)} %bitcast.7), custom_call_target="tpu_custom_call" | custom-call | tf_op jit(solution)/shard_map/self_energy/pallas_call | solution.py:379
  45.9 1.1 %copy.11 = f32[1,4]{1,0:T(1,128)} copy(f32[1,4]{1,0:T(1,128)} %self_energy.1) | data formatting | bytes 32

commit v2 on v1

--- a/solution.py
+++ b/solution.py
@@ -13,7 +13,6 @@
 NB = 32
 LANES = 128
 SLOTS = 16
-V_EARLY = 16
 MESH = pl.DeviceIdType.MESH
 BF = jnp.bfloat16
 F32 = jnp.float32
@@ -39,12 +38,13 @@
 
 def body(
     np_, ka, ql,
-    coup, vec, ener, kc, rc, deg, kq, om, ph,
+    coup, vec_in, ener_in, kc_in, rc_in, deg_in, kq_in, om_in, ph_in,
     out,
-    xbuf, sums, sendc, recvc, sendz, recvz, vsend, vgot, esend, egot,
+    vec, ener, kc, rc, deg, kq, om, ph,
+    xbuf, sums, sendc, recvc, sendz, recvz, vsend, vrows, esend, egot,
     flat, posend, pogot, kqsend, kqgot, kqs, spread, phx, fold, fsend, fgot,
-    turned, vq, occ, eq,
-    xsem, csem, zsend, zrecv, vs_sem, vr_sem, es_sem, er_sem, wsem,
+    slots, shifts, raw, vq, occ, small_sem,
+    xsem, csem, zsend, zrecv, vs_sem, vr_sem, es_sem, er_sem, wsem, vp_send, vp_recv,
     ps_sem, pr_sem, ks_sem, kr_sem, ksm, fs_sem, fr_sem,
 ):
     ni = ka // 2
@@ -73,11 +73,12 @@
     def mate(o):
         return lax.rem(mp + 1 + o, np_)
 
-    def each(count, f):
+    def each(count, f, unroll=True):
         def step(o, carry):
             f(o)
             return carry
-        lax.fori_loop(0, count, step, 0)
+        if count:
+            lax.fori_loop(0, count, step, 0, unroll=unroll)
 
     barrier = pltpu.get_barrier_semaphore()
     each(ni - 1, lambda o: pl.semaphore_signal(
@@ -86,8 +87,16 @@
     each(np_ - 1, lambda o: pl.semaphore_signal(
         barrier, inc=1, device_id={"pb": mate(o)}, device_id_type=MESH))
 
+    loads = [pltpu.make_async_copy(src, dst, small_sem.at[n]) for n, (src, dst) in enumerate([
+        (kc_in, kc), (rc_in, rc), (deg_in, deg), (vec_in, vec), (ener_in, ener), (kq_in, kq), (om_in, om), (ph_in, ph)])]
+    for c in loads[:3]:
+        c.start()
     load = pltpu.make_async_copy(coup, xbuf, xsem)
     load.start()
+    for c in loads[3:]:
+        c.start()
+    for c in loads[:3]:
+        c.wait()
 
     kpad = jnp.concatenate(
         [kc[...].astype(F32), jnp.zeros((5, ka), F32)], axis=0)
@@ -107,7 +116,7 @@
     sine = jnp.where(odd, cos_a, sin_a)
     cosine = jnp.where((quad == 1.0) | (quad == 2.0), -cosine, cosine)
     sine = jnp.where((quad == 2.0) | (quad == 3.0), -sine, sine)
-    inverse = 1.0 / deg[...].astype(F32)
+    inverse = 1.0 / deg[...].reshape(1, rl).astype(F32)
     both = jnp.concatenate([cosine * inverse, sine * inverse], axis=0).astype(BF)
 
     load.wait()
@@ -135,6 +144,8 @@
         sendc[i] = of_point(2 * i + (1 - mc)).astype(BF)
     each(ni, to_partner)
 
+    for c in loads[3:]:
+        c.wait()
     lane8 = iota((8, LANES), 1)
     v = vec[...]
     vsend[...] = v.astype(BF)
@@ -172,23 +183,32 @@
     pogot[mp] = posend[...]
     kqgot[mp] = kqsend[...]
 
+    nj = ni // np_
+
     def e_copy(o, i):
-        return copy(esend, egot.at[mc, mi], es_sem.at[o], er_sem.at[mi], {"ka": i * 2 + mc})
-
-    def v_copy(o, i):
-        return copy(vsend, vgot.at[mc, mi], vs_sem.at[o], vr_sem.at[mi], {"ka": i * 2 + mc})
+        return copy(esend, egot.at[mc * ni + mi], es_sem.at[o], er_sem.at[mi], {"ka": i * 2 + mc})
+
+    def v_slot(j):
+        return vrows.at[mc * ni + mp * nj + j]
+
+    def v_copy(j, i):
+        return copy(vsend, v_slot(j), vs_sem.at[j], vr_sem.at[j], {"ka": i * 2 + mc})
 
     def z_copy(o, i):
         return copy(sendz.at[i], recvz.at[mi], zsend.at[o], zrecv.at[mi], {"ka": i * 2 + mc})
 
-    early = min(V_EARLY, ni - 1)
-
-    def first(o):
-        v_copy(o, chip(o)).start()
-    each(early, first)
+    last = mp == np_ - 1
+    each(nj - 1, lambda j: v_copy(j, chip(mp + np_ * j)).start())
+
+    @pl.when(jnp.logical_not(last))
+    def _():
+        v_copy(nj - 1, chip(mp + np_ * (nj - 1))).start()
+
+    @pl.when(last)
+    def _():
+        vrows[mc * ni + mp * nj + nj - 1] = vsend[...]
     each(ni - 1, lambda o: e_copy(o, chip(o)).start())
-    vgot[mc, mi] = vsend[...]
-    egot[mc, mi] = esend[...]
+    egot[mc * ni + mi] = esend[...]
 
     swap.wait_recv()
 
@@ -198,10 +218,6 @@
         z_copy(o, i).start()
     each(ni - 1, add_and_send)
     own = of_point(me) + recvc[mi].astype(F32)
-
-    def late(o):
-        v_copy(o + early, chip(o + early)).start()
-    each(ni - 1 - early, late)
 
     for blk, (s0, c0, s1, c1) in enumerate(
         [(1, 0, 1, 1), (-1, 1, 1, 0), (1, 1, -1, 0), (1, 0, 1, 1)]
@@ -220,6 +236,10 @@
 
     q_at = iota((LANES, width), 1) // NB
     spread[...] = ((q_at // ql) * SLOTS + q_at % ql == iota((LANES, width), 0)).astype(F32).astype(BF)
+
+    r_at, c_at = iota((512, 512), 0), iota((512, 512), 1)
+    same = (r_at // LANES == (c_at // NB) % 4) & ((r_at // NB) % 4 == c_at // LANES) & (r_at % NB == c_at % NB)
+    shifts[...] = same.astype(F32).astype(BF)
 
     def small_wait(o):
         src = mate(o)
@@ -243,11 +263,70 @@
         phx[:, at] = total
     to_scalar.wait()
 
+    def v_arrived(j):
+        copy(vsend, v_slot(j), vs_sem.at[j], vr_sem.at[j], {"ka": me}).wait_recv()
+
+    each(nj - 1, v_arrived)
+
+    @pl.when(jnp.logical_not(last))
+    def _():
+        v_arrived(nj - 1)
+
+    def v_block(p, c):
+        return vrows.at[pl.ds(c * ni + p * nj, nj)]
+
+    def vp_copy(o, p, to):
+        return copy(v_block(p, mc), v_block(p, mc), vp_send.at[o], vp_recv.at[p], {"pb": to})
+    each(np_ - 1, lambda o: vp_copy(o, mp, mate(o)).start())
+
+    def find(q):
+        point = kqs[q // ql, 0, lax.rem(q, ql)]
+        c, i = lax.rem(point, 2), point // 2
+        dz = lax.rem(mz - i // 2 + nz, nz) - nz // 2
+        dy = lax.rem(my - lax.rem(i, 2) + 2, 2)
+        o = 2 * jnp.where(dz >= 0, 2 * dz, -2 * dz - 1) + 1 - dy
+        slots[0, q] = c * ni + lax.rem(o, np_) * nj + o // np_
+        slots[1, q] = c * ni + i
+    each(queries, find, unroll=4)
+
+    def e_wait(o):
+        i = chip(o)
+        copy(esend, egot.at[mc * ni + i], es_sem.at[o], er_sem.at[i], {"ka": i * 2 + mc}).wait_recv()
+    each(ni - 1, e_wait)
+
+    def e_half(c):
+        return egot.at[pl.ds(c * ni, ni)]
+    give_e = copy(e_half(mc), e_half(mc), wsem.at[2], wsem.at[3], other)
+    give_e.start()
+    copy(e_half(1 - mc), e_half(1 - mc), wsem.at[2], wsem.at[3], other).wait_recv()
+
+    lane1 = iota((1, LANES), 1) // NB
+    row_e = iota((rows, LANES), 0) % nb + mp * nb
+    e_col = jnp.sum(
+        jnp.where(iota((rows, LANES), 1) == row_e, esend[...], 0.0), axis=1, keepdims=True)
+
+    def occupations(t):
+        at = pl.ds(pl.multiple_of(t * LANES, LANES), LANES)
+        e4 = [egot[slots[1, 4 * t + g]] for g in range(4)]
+        e_there = jnp.where(lane1 < 2, jnp.where(lane1 == 0, e4[0], e4[1]), jnp.where(lane1 == 2, e4[2], e4[3]))
+        fermi = 1.0 / (1.0 + jnp.exp(e_there * (1.0 / THERMAL)))
+        gap = e_col - e_there
+        omega = phx[64 : 64 + np_, at]
+        bose = 1.0 / (jnp.exp(omega * (1.0 / THERMAL)) - 1.0)
+        scale = SMEARING / (math.pi * queries)
+        for m in range(np_):
+            w, b = omega[m : m + 1], bose[m : m + 1]
+            up, down = gap + w, gap - w
+            value = (b + fermi) * (scale / (up * up + SMEARING * SMEARING))
+            value += (b + 1.0 - fermi) * (scale / (down * down + SMEARING * SMEARING))
+            occ[m, :, at] = value
+    each(tiles, occupations, unroll=2)
+
     def z_wait(o, total):
         i = chip(o)
         copy(sendz.at[i], recvz.at[i], zsend.at[o], zrecv.at[i], {"ka": i * 2 + mc}).wait_recv()
         return total + recvz[i].astype(F32)
-    wann = lax.fori_loop(0, ni - 1, z_wait, own).astype(BF).astype(F32)
+    wann = lax.fori_loop(0, ni - 1, z_wait, own, unroll=True).astype(BF).astype(F32)
     blocks = []
     for low in range(4):
         for part in range(2):
@@ -269,61 +348,48 @@
     each(np_ - 1, lambda o: f_copy(o, mate(o)).start())
     fgot[mp] = fsend[mp]
 
-    def v_wait(o):
+    def vp_wait(o):
+        src = mate(o)
+        vp_copy(o, src, src).wait_recv()
+    each(np_ - 1, vp_wait)
+
+    def v_half(c):
+        return vrows.at[pl.ds(c * ni, ni)]
+    give_v = copy(v_half(mc), v_half(mc), wsem.at[0], wsem.at[1], other)
+    give_v.start()
+
+    swap.wait_send()
+    give_e.wait_send()
+
+    def drain(o):
         i = chip(o)
-        copy(vsend, vgot.at[mc, i], vs_sem.at[o], vr_sem.at[i], {"ka": i * 2 + mc}).wait_recv()
-        copy(esend, egot.at[mc, i], es_sem.at[o], er_sem.at[i], {"ka": i * 2 + mc}).wait_recv()
-    each(ni - 1, v_wait)
-    give_v = copy(vgot.at[mc], vgot.at[mc], wsem.at[0], wsem.at[1], other)
-    give_e = copy(egot.at[mc], egot.at[mc], wsem.at[2], wsem.at[3], other)
-    give_v.start()
-    give_e.start()
-
-    def rolled(c):
-        def step(i):
-            val = vgot[c, i].astype(F32)
-            turned[0, c, i] = val
-            for s in range(1, 4):
-                turned[s, c, i] = spin(val, 32 * s)
-        each(ni, step)
-    rolled(mc)
-    copy(vgot.at[1 - mc], vgot.at[1 - mc], wsem.at[0], wsem.at[1], other).wait_recv()
-    copy(egot.at[1 - mc], egot.at[1 - mc], wsem.at[2], wsem.at[3], other).wait_recv()
-    rolled(1 - mc)
-
-    lane16 = iota((16, LANES), 1) // NB
-    lane1 = iota((1, LANES), 1) // NB
-    row_e = iota((rows, LANES), 0) % nb + mp * nb
-    e_col = jnp.sum(
-        jnp.where(iota((rows, LANES), 1) == row_e, esend[...], 0.0), axis=1, keepdims=True)
-
-    def by_group(mask, vals):
-        return jnp.where(mask == 0, vals[0], jnp.where(
-            mask == 1, vals[1], jnp.where(mask == 2, vals[2], vals[3])))
-
-    def tables(t):
-        at = pl.ds(pl.multiple_of(t * LANES, LANES), LANES)
-        where = []
+        z_copy(o, i).wait_send()
+        e_copy(o, i).wait_send()
+    each(ni - 1, drain)
+    each(nj - 1, lambda j: v_copy(j, chip(mp + np_ * j)).wait_send())
+
+    @pl.when(jnp.logical_not(last))
+    def _():
+        v_copy(nj - 1, chip(mp + np_ * (nj - 1))).wait_send()
+
+    def drain_small(o):
+        po_copy(o, mate(o)).wait_send()
+        kq_copy(o, mate(o)).wait_send()
+        vp_copy(o, mp, mate(o)).wait_send()
+    each(np_ - 1, drain_small)
+
+    copy(v_half(1 - mc), v_half(1 - mc), wsem.at[0], wsem.at[1], other).wait_recv()
+
+    def take(t):
         for g in range(4):
-            q = 4 * t + g
-            point = kqs[q // ql, 0, lax.rem(q, ql)]
-            where.append((lax.rem(point, 2), point // 2))
-        for low in range(4):
-            vq[16 * low : 16 * low + 16, at] = by_group(
-                lane16, [turned[(g - low) % 4, where[g][0], where[g][1]] for g in range(4)]).astype(BF)
-        e_there = by_group(lane1, [egot[where[g][0], where[g][1]] for g in range(4)])
-        fermi = 1.0 / (1.0 + jnp.exp(e_there * (1.0 / THERMAL)))
-        gap = e_col - e_there
-        omega = phx[64:72, at]
-        bose = 1.0 / (jnp.exp(omega * (1.0 / THERMAL)) - 1.0)
-        for m in range(np_):
-            w, b = omega[m : m + 1], bose[m : m + 1]
-            up, down = gap + w, gap - w
-            scale = SMEARING / (math.pi * queries)
-            value = (b + fermi) * (scale / (up * up + SMEARING * SMEARING))
-            value += (b + 1.0 - fermi) * (scale / (down * down + SMEARING * SMEARING))
-            occ[m, :, at] = value
-    each(tiles, tables)
+            raw[pl.ds(pl.multiple_of(t * 16, 16), 16), g * LANES : (g + 1) * LANES] = vrows[slots[0, 4 * t + g]]
+    each(tiles, take, unroll=4)
+    for h in range(2):
+        moved = jnp.dot(raw[...], shifts[:, 256 * h : 256 * h + 256], preferred_element_type=F32).astype(BF)
+        for low in range(2):
+            for t in range(tiles):
+                vq[32 * h + 16 * low : 32 * h + 16 * low + 16, t * LANES : (t + 1) * LANES] = moved[
+                    16 * t : 16 * t + 16, low * LANES : (low + 1) * LANES]
 
     def f_wait(o):
         src = mate(o)
@@ -340,28 +406,14 @@
                 g += phx[w * np_ + m : w * np_ + m + 1, at] * h[w * rows : (w + 1) * rows]
             total += (g * g) * occ[m, :, at]
         return total
-    total = lax.fori_loop(0, width // 256, finish, jnp.zeros((rows, 256), F32))
+    total = lax.fori_loop(0, width // 256, finish, jnp.zeros((rows, 256), F32), unroll=True)
     summed = jnp.sum(total, axis=1, keepdims=True)
     out[...] = jnp.sum(
         jnp.where(iota((rows, LANES), 1) == iota((rows, LANES), 0) % nb, summed, 0.0),
         axis=0, keepdims=True)[:, :nb]
 
-    swap.wait_send()
     give_v.wait_send()
-    give_e.wait_send()
-
-    def drain(o):
-        i = chip(o)
-        z_copy(o, i).wait_send()
-        v_copy(o, i).wait_send()
-        e_copy(o, i).wait_send()
-    each(ni - 1, drain)
-
-    def drain_small(o):
-        po_copy(o, mate(o)).wait_send()
-        kq_copy(o, mate(o)).wait_send()
-        f_copy(o, mate(o)).wait_send()
-    each(np_ - 1, drain_small)
+    each(np_ - 1, lambda o: f_copy(o, mate(o)).wait_send())
 
 
 def shards(mesh, coupling, eigvec, energies, k_coords, r_coords, degeneracy, kq_index, omega, phonon_modes):
@@ -379,9 +431,17 @@
     return pl.pallas_call(
         functools.partial(body, np_, ka, ql),
         out_shape=jax.ShapeDtypeStruct((1, nb), F32),
-        in_specs=[hbm] + [vm] * 8,
+        in_specs=[hbm] * 9,
         out_specs=vm,
         scratch_shapes=[
+            V((16, LANES), F32),
+            V((1, NB), F32),
+            V((3, ka), jnp.int32),
+            V((3, rl), jnp.int32),
+            V((rl,), jnp.int32),
+            V((1, ql), jnp.int32),
+            V((np_, ql), F32),
+            V((np_ * np_, ql), F32),
             V((rl, 2048), BF),
             V((16 * ka, LANES), F32),
             V((ni, 16, LANES), BF),
@@ -389,9 +449,9 @@
             V((ni, 16, LANES), BF),
             V((ni, 16, LANES), BF),
             V((16, LANES), BF),
-            V((2, ni, 16, LANES), BF),
+            V((2 * ni, 16, LANES), BF),
             V((1, LANES), F32),
-            V((2, ni, 1, LANES), F32),
+            V((2 * ni, 1, LANES), F32),
             V((LANES, LANES), F32),
             V((SLOTS, LANES), F32),
             V((np_, SLOTS, LANES), F32),
@@ -403,11 +463,13 @@
             V((64, 256), BF),
             V((np_, rows, LANES), F32),
             V((np_, rows, LANES), F32),
-            V((4, 2, ni, 16, LANES), F32),
+            pltpu.SMEM((2, ql * np_), jnp.int32),
+            V((512, 512), BF),
+            V((width // 8, 512), BF),
             V((64, width), BF),
             V((np_, rows, width), F32),
-            V((1, LANES), F32),
-            sem, sem((2,)), sem((ni,)), sem((ni,)), sem((ni,)), sem((ni,)), sem((ni,)), sem((ni,)), sem((4,)),
+            sem((8,)),
+            sem, sem((2,)), sem((ni,)), sem((ni,)), sem((ni,)), sem((ni,)), sem((ni,)), sem((ni,)), sem((4,)), sem((np_,)), sem((np_,)),
             sem((np_,)), sem((np_,)), sem((np_,)), sem((np_,)), sem, sem((np_,)), sem((np_,)),
         ],
         compiler_params=pltpu.CompilerParams(collective_id=0, has_side_effects=True),
@@ -418,7 +480,7 @@
         energies,
         k_coords,
         r_coords,
-        degeneracy.reshape(1, rl),
+        degeneracy,
         kq_index,
         omega.T,
         jnp.transpose(phonon_modes, (1, 2, 0)).reshape(np_ * np_, ql),

time: 47.3 us -> 37.4 us (0.79)
  Pallas kernels: 44.7 us -> 36 us
  local copies, waits for them, and re-layouts: 2.38 us -> 1.19 us
    pallas_call x1, Pallas kernels: 44.7 us -> 36 us  [shards(): pl.pallas_call(functools.partial(body, np_, ka, ql), out_shape=jax.ShapeD...]
    reshape x1 -> x0, local copies, waits for them, and re-layouts: 1.27 us -> none  [shards(): degeneracy.reshape(1, rl)]
where the time goes in v2:
time: 37.4 us; the launch traced here: 37.2 us
  Pallas kernels  36 us (96%)
  local copies, waits for them, and re-layouts  1.19 us (3%)
    pallas_call x1, Pallas kernels, shards(): pl.pallas_call(functools.partial(body, np_, ka, ql), out_shape=jax.ShapeD...  36 us
    unnamed x1, local copies, waits for them, and re-layouts  1.19 us

profile of v2, /device:TPU:1, one launch (start us, length us, event | category | flops | bytes accessed | tf_op | source)
XLA Modules:
  0.0 37.2 jit_solution(8686555507654007384)
XLA Ops:
  0.0 36.0 %self_energy.1 = f32[1,4]{1,0:T(1,128)} custom-call(bf16[320,2048]{1,0:T(8,128)(2,1)} %bitcast.6, f32[16,128]{1,0:T(8,128)} %bitcast.8, f32[1,32]{1,0:T(1,128)} %ener_in.1, s32[3,64]{1,0:T(4,128)} %kc_in.1, s32[3,320]{1,0:T(4,128)} %rc_in.1, s32[320]{0:T(512)} %deg_in.1, s32[1,12]{1,0:T(1,128)} %kq_in.1, f32[8,12]{1,0:T(8,128)} %bitcast.9, f32[64,12]{1,0:T(8,128)} %bitcast.7), custom_call_target="tpu_custom_call" | custom-call | tf_op jit(solution)/shard_map/self_energy/pallas_call | solution.py:431
  36.0 1.2 %copy.11 = f32[1,4]{1,0:T(1,128)} copy(f32[1,4]{1,0:T(1,128)} %self_energy.1) | data formatting | bytes 32

commit v3 on v2

--- a/solution.py
+++ b/solution.py
@@ -44,8 +44,7 @@
     xbuf, sums, sendc, recvc, sendz, recvz, vsend, vrows, esend, egot,
     flat, posend, pogot, kqsend, kqgot, kqs, spread, phx, fold, fsend, fgot,
     slots, shifts, raw, vq, occ, small_sem,
-    xsem, csem, zsend, zrecv, vs_sem, vr_sem, es_sem, er_sem, wsem, vp_send, vp_recv,
-    ps_sem, pr_sem, ks_sem, kr_sem, ksm, fs_sem, fr_sem,
+    xsem, csem, wsem, ksm, sems,
 ):
     ni = ka // 2
     nz = ni // 2
@@ -167,14 +166,18 @@
         return pltpu.make_async_remote_copy(
             src_ref=src, dst_ref=dst, send_sem=s, recv_sem=r, device_id=to, device_id_type=MESH)
 
+    def all_of(ref, count, sem):
+        part = ref.at[pl.ds(0, count)]
+        pltpu.make_async_copy(part, part, sem).wait()
+
     swap = copy(sendc, recvc, csem.at[0], csem.at[1], other)
     swap.start()
 
     def po_copy(o, to):
-        return copy(posend, pogot.at[mp], ps_sem.at[o], pr_sem.at[mp], {"pb": to})
+        return copy(posend, pogot.at[mp], sems.at[0], sems.at[1], {"pb": to})
 
     def kq_copy(o, to):
-        return copy(kqsend, kqgot.at[mp], ks_sem.at[o], kr_sem.at[mp], {"pb": to})
+        return copy(kqsend, kqgot.at[mp], sems.at[2], sems.at[3], {"pb": to})
 
     def small(o):
         po_copy(o, mate(o)).start()
@@ -186,16 +189,16 @@
     nj = ni // np_
 
     def e_copy(o, i):
-        return copy(esend, egot.at[mc * ni + mi], es_sem.at[o], er_sem.at[mi], {"ka": i * 2 + mc})
+        return copy(esend, egot.at[mc * ni + mi], sems.at[4], sems.at[5], {"ka": i * 2 + mc})
 
     def v_slot(j):
         return vrows.at[mc * ni + mp * nj + j]
 
     def v_copy(j, i):
-        return copy(vsend, v_slot(j), vs_sem.at[j], vr_sem.at[j], {"ka": i * 2 + mc})
+        return copy(vsend, v_slot(j), sems.at[6], sems.at[7], {"ka": i * 2 + mc})
 
     def z_copy(o, i):
-        return copy(sendz.at[i], recvz.at[mi], zsend.at[o], zrecv.at[mi], {"ka": i * 2 + mc})
+        return copy(sendz.at[i], recvz.at[mi], sems.at[8], sems.at[9], {"ka": i * 2 + mc})
 
     last = mp == np_ - 1
     each(nj - 1, lambda j: v_copy(j, chip(mp + np_ * j)).start())
@@ -241,13 +244,8 @@
     same = (r_at // LANES == (c_at // NB) % 4) & ((r_at // NB) % 4 == c_at // LANES) & (r_at % NB == c_at % NB)
     shifts[...] = same.astype(F32).astype(BF)
 
-    def small_wait(o):
-        src = mate(o)
-        po_in = copy(posend, pogot.at[src], ps_sem.at[o], pr_sem.at[src], {"pb": src})
-        po_in.wait_recv()
-        kq_in = copy(kqsend, kqgot.at[src], ks_sem.at[o], kr_sem.at[src], {"pb": src})
-        kq_in.wait_recv()
-    each(np_ - 1, small_wait)
+    all_of(pogot, np_ - 1, sems.at[1])
+    all_of(kqgot, np_ - 1, sems.at[3])
     to_scalar = pltpu.make_async_copy(kqgot, kqs, ksm)
     to_scalar.start()
     got = pogot[...].reshape(np_ * SLOTS, LANES)
@@ -263,36 +261,31 @@
         phx[:, at] = total
     to_scalar.wait()
 
-    def v_arrived(j):
-        copy(vsend, v_slot(j), vs_sem.at[j], vr_sem.at[j], {"ka": me}).wait_recv()
-
-    each(nj - 1, v_arrived)
-
     @pl.when(jnp.logical_not(last))
     def _():
-        v_arrived(nj - 1)
+        all_of(vrows, nj, sems.at[7])
+
+    @pl.when(last)
+    def _():
+        all_of(vrows, nj - 1, sems.at[7])
 
     def v_block(p, c):
         return vrows.at[pl.ds(c * ni + p * nj, nj)]
 
     def vp_copy(o, p, to):
-        return copy(v_block(p, mc), v_block(p, mc), vp_send.at[o], vp_recv.at[p], {"pb": to})
+        return copy(v_block(p, mc), v_block(p, mc), sems.at[10], sems.at[11], {"pb": to})
     each(np_ - 1, lambda o: vp_copy(o, mp, mate(o)).start())
 
-    def find(q):
-        point = kqs[q // ql, 0, lax.rem(q, ql)]
+    for q in range(queries):
+        point = kqs[q // ql, 0, q % ql]
         c, i = lax.rem(point, 2), point // 2
         dz = lax.rem(mz - i // 2 + nz, nz) - nz // 2
         dy = lax.rem(my - lax.rem(i, 2) + 2, 2)
         o = 2 * jnp.where(dz >= 0, 2 * dz, -2 * dz - 1) + 1 - dy
         slots[0, q] = c * ni + lax.rem(o, np_) * nj + o // np_
         slots[1, q] = c * ni + i
-    each(queries, find, unroll=4)
-
-    def e_wait(o):
-        i = chip(o)
-        copy(esend, egot.at[mc * ni + i], es_sem.at[o], er_sem.at[i], {"ka": i * 2 + mc}).wait_recv()
-    each(ni - 1, e_wait)
+
+    all_of(egot, ni - 1, sems.at[5])
 
     def e_half(c):
         return egot.at[pl.ds(c * ni, ni)]
@@ -322,11 +315,11 @@
             occ[m, :, at] = value
     each(tiles, occupations, unroll=2)
 
-    def z_wait(o, total):
-        i = chip(o)
-        copy(sendz.at[i], recvz.at[i], zsend.at[o], zrecv.at[i], {"ka": i * 2 + mc}).wait_recv()
-        return total + recvz[i].astype(F32)
-    wann = lax.fori_loop(0, ni - 1, z_wait, own, unroll=True).astype(BF).astype(F32)
+    all_of(recvz, ni - 1, sems.at[9])
+    terms = [own] + [recvz[chip(o)].astype(F32) for o in range(ni - 1)]
+    while len(terms) > 1:
+        terms = [terms[n] + terms[n + 1] for n in range(0, len(terms) - 1, 2)] + terms[len(terms) & ~1 :]
+    wann = terms[0].astype(BF).astype(F32)
     blocks = []
     for low in range(4):
         for part in range(2):
@@ -344,14 +337,11 @@
         fsend[p] = folded[p * rows : (p + 1) * rows]
 
     def f_copy(o, to):
-        return copy(fsend.at[to], fgot.at[mp], fs_sem.at[o], fr_sem.at[mp], {"pb": to})
+        return copy(fsend.at[to], fgot.at[mp], sems.at[12], sems.at[13], {"pb": to})
     each(np_ - 1, lambda o: f_copy(o, mate(o)).start())
     fgot[mp] = fsend[mp]
 
-    def vp_wait(o):
-        src = mate(o)
-        vp_copy(o, src, src).wait_recv()
-    each(np_ - 1, vp_wait)
+    all_of(vrows, (np_ - 1) * nj, sems.at[11])
 
     def v_half(c):
         return vrows.at[pl.ds(c * ni, ni)]
@@ -361,22 +351,19 @@
     swap.wait_send()
     give_e.wait_send()
 
-    def drain(o):
-        i = chip(o)
-        z_copy(o, i).wait_send()
-        e_copy(o, i).wait_send()
-    each(ni - 1, drain)
-    each(nj - 1, lambda j: v_copy(j, chip(mp + np_ * j)).wait_send())
+    all_of(sendz, ni - 1, sems.at[8])
+    all_of(egot, ni - 1, sems.at[4])
 
     @pl.when(jnp.logical_not(last))
     def _():
-        v_copy(nj - 1, chip(mp + np_ * (nj - 1))).wait_send()
-
-    def drain_small(o):
-        po_copy(o, mate(o)).wait_send()
-        kq_copy(o, mate(o)).wait_send()
-        vp_copy(o, mp, mate(o)).wait_send()
-    each(np_ - 1, drain_small)
+        all_of(vrows, nj, sems.at[6])
+
+    @pl.when(last)
+    def _():
+        all_of(vrows, nj - 1, sems.at[6])
+    all_of(pogot, np_ - 1, sems.at[0])
+    all_of(kqgot, np_ - 1, sems.at[2])
+    all_of(vrows, (np_ - 1) * nj, sems.at[10])
 
     copy(v_half(1 - mc), v_half(1 - mc), wsem.at[0], wsem.at[1], other).wait_recv()
 
@@ -391,10 +378,7 @@
                 vq[32 * h + 16 * low : 32 * h + 16 * low + 16, t * LANES : (t + 1) * LANES] = moved[
                     16 * t : 16 * t + 16, low * LANES : (low + 1) * LANES]
 
-    def f_wait(o):
-        src = mate(o)
-        copy(fsend.at[src], fgot.at[src], fs_sem.at[o], fr_sem.at[src], {"pb": src}).wait_recv()
-    each(np_ - 1, f_wait)
+    all_of(fgot, np_ - 1, sems.at[13])
     left = fgot[...].reshape(np_ * rows, LANES)[:, :64].astype(BF)
 
     def finish(t, total):
@@ -413,7 +397,7 @@
         axis=0, keepdims=True)[:, :nb]
 
     give_v.wait_send()
-    each(np_ - 1, lambda o: f_copy(o, mate(o)).wait_send())
+    all_of(fgot, np_ - 1, sems.at[12])
 
 
 def shards(mesh, coupling, eigvec, energies, k_coords, r_coords, degeneracy, kq_index, omega, phonon_modes):
@@ -469,8 +453,7 @@
             V((64, width), BF),
             V((np_, rows, width), F32),
             sem((8,)),
-            sem, sem((2,)), sem((ni,)), sem((ni,)), sem((ni,)), sem((ni,)), sem((ni,)), sem((ni,)), sem((4,)), sem((np_,)), sem((np_,)),
-            sem((np_,)), sem((np_,)), sem((np_,)), sem((np_,)), sem, sem((np_,)), sem((np_,)),
+            sem, sem((2,)), sem((4,)), sem, sem((14,)),
         ],
         compiler_params=pltpu.CompilerParams(collective_id=0, has_side_effects=True),
         name="self_energy",

time: 37.4 us -> 34.8 us (0.930)
  Pallas kernels: 36 us -> 33.4 us
    pallas_call x1, Pallas kernels: 36 us -> 33.4 us  [shards(): pl.pallas_call(functools.partial(body, np_, ka, ql), out_shape=jax.ShapeD...]
where the time goes in v3:
time: 34.8 us; the launch traced here: 34.6 us
  Pallas kernels  33.4 us (96%)
  local copies, waits for them, and re-layouts  1.19 us (3%)
    pallas_call x1, Pallas kernels, shards(): pl.pallas_call(functools.partial(body, np_, ka, ql), out_shape=jax.ShapeD...  33.4 us
    unnamed x1, local copies, waits for them, and re-layouts  1.19 us

profile of v3, /device:TPU:1, one launch (start us, length us, event | category | flops | bytes accessed | tf_op | source)
XLA Modules:
  0.0 34.6 jit_solution(15309768025761153660)
XLA Ops:
  0.0 33.4 %self_energy.1 = f32[1,4]{1,0:T(1,128)} custom-call(bf16[320,2048]{1,0:T(8,128)(2,1)} %bitcast.6, f32[16,128]{1,0:T(8,128)} %bitcast.8, f32[1,32]{1,0:T(1,128)} %ener_in.1, s32[3,64]{1,0:T(4,128)} %kc_in.1, s32[3,320]{1,0:T(4,128)} %rc_in.1, s32[320]{0:T(512)} %deg_in.1, s32[1,12]{1,0:T(1,128)} %kq_in.1, f32[8,12]{1,0:T(8,128)} %bitcast.9, f32[64,12]{1,0:T(8,128)} %bitcast.7), custom_call_target="tpu_custom_call" | custom-call | tf_op jit(solution)/shard_map/self_energy/pallas_call | solution.py:415
  33.4 1.2 %copy.11 = f32[1,4]{1,0:T(1,128)} copy(f32[1,4]{1,0:T(1,128)} %self_energy.1) | data formatting | bytes 32

commit v4 on v3

--- a/solution.py
+++ b/solution.py
@@ -414,7 +414,7 @@
     sem = pltpu.SemaphoreType.DMA
     return pl.pallas_call(
         functools.partial(body, np_, ka, ql),
-        out_shape=jax.ShapeDtypeStruct((1, nb), F32),
+        out_shape=pltpu.VMEM((1, nb), F32),
         in_specs=[hbm] * 9,
         out_specs=vm,
         scratch_shapes=[

time: 34.8 us -> 33.5 us (0.963)
  local copies, waits for them, and re-layouts: 1.19 us -> 0.51 us
  Pallas kernels: 33.4 us -> 32.8 us
    unnamed x1, local copies, waits for them, and re-layouts: 1.19 us -> 0.51 us
    pallas_call x1, Pallas kernels: 33.4 us -> 32.8 us  [shards(): pl.pallas_call(functools.partial(body, np_, ka, ql), out_shape=pltpu.VMEM...]
where the time goes in v4:
time: 33.5 us; the launch traced here: 33.4 us
  Pallas kernels  32.8 us (98%)
  local copies, waits for them, and re-layouts  0.51 us (2%)
    pallas_call x1, Pallas kernels, shards(): pl.pallas_call(functools.partial(body, np_, ka, ql), out_shape=pltpu.VMEM...  32.8 us

profile of v4, /device:TPU:1, one launch (start us, length us, event | category | flops | bytes accessed | tf_op | source)
XLA Modules:
  0.0 33.4 jit_solution(13641654190567393015)
XLA Ops:
  0.0 32.8 %self_energy.1 = f32[1,4]{1,0:T(1,128)S(1)} custom-call(bf16[320,2048]{1,0:T(8,128)(2,1)} %bitcast.6, f32[16,128]{1,0:T(8,128)} %bitcast.8, f32[1,32]{1,0:T(1,128)} %ener_in.1, s32[3,64]{1,0:T(4,128)} %kc_in.1, s32[3,320]{1,0:T(4,128)} %rc_in.1, s32[320]{0:T(512)} %deg_in.1, s32[1,12]{1,0:T(1,128)} %kq_in.1, f32[8,12]{1,0:T(8,128)} %bitcast.9, f32[64,12]{1,0:T(8,128)} %bitcast.7), custom_call_target="tpu_custom_call" | custom-call | tf_op jit(solution)/shard_map/self_energy/pallas_call | solution.py:415
  32.8 0.5 %copy.11 = f32[1,4]{1,0:T(1,128)} copy(f32[1,4]{1,0:T(1,128)S(1)} %self_energy.1) | data formatting | bytes 32

commit v5 on v4

--- a/solution.py
+++ b/solution.py
@@ -69,6 +69,14 @@
         y = lax.rem(my + 1 - lax.rem(o, 2), 2)
         return z * 2 + y
 
+    def in_z_order(f):
+        for z in range(nz):
+            f(z * 2 + 1 - my)
+
+            @pl.when(mz != z)
+            def _():
+                f(z * 2 + my)
+
     def mate(o):
         return lax.rem(mp + 1 + o, np_)
 
@@ -210,16 +218,15 @@
     @pl.when(last)
     def _():
         vrows[mc * ni + mp * nj + nj - 1] = vsend[...]
-    each(ni - 1, lambda o: e_copy(o, chip(o)).start())
+    in_z_order(lambda i: e_copy(0, i).start())
     egot[mc * ni + mi] = esend[...]
 
     swap.wait_recv()
 
-    def add_and_send(o):
-        i = chip(o)
+    def add_and_send(i):
         sendz[i] = (of_point(2 * i + mc) + recvc[i].astype(F32)).astype(BF)
-        z_copy(o, i).start()
-    each(ni - 1, add_and_send)
+        z_copy(0, i).start()
+    in_z_order(add_and_send)
     own = of_point(me) + recvc[mi].astype(F32)
 
     for blk, (s0, c0, s1, c1) in enumerate(
@@ -291,29 +298,6 @@
         return egot.at[pl.ds(c * ni, ni)]
     give_e = copy(e_half(mc), e_half(mc), wsem.at[2], wsem.at[3], other)
     give_e.start()
-    copy(e_half(1 - mc), e_half(1 - mc), wsem.at[2], wsem.at[3], other).wait_recv()
-
-    lane1 = iota((1, LANES), 1) // NB
-    row_e = iota((rows, LANES), 0) % nb + mp * nb
-    e_col = jnp.sum(
-        jnp.where(iota((rows, LANES), 1) == row_e, esend[...], 0.0), axis=1, keepdims=True)
-
-    def occupations(t):
-        at = pl.ds(pl.multiple_of(t * LANES, LANES), LANES)
-        e4 = [egot[slots[1, 4 * t + g]] for g in range(4)]
-        e_there = jnp.where(lane1 < 2, jnp.where(lane1 == 0, e4[0], e4[1]), jnp.where(lane1 == 2, e4[2], e4[3]))
-        fermi = 1.0 / (1.0 + jnp.exp(e_there * (1.0 / THERMAL)))
-        gap = e_col - e_there
-        omega = phx[64 : 64 + np_, at]
-        bose = 1.0 / (jnp.exp(omega * (1.0 / THERMAL)) - 1.0)
-        scale = SMEARING / (math.pi * queries)
-        for m in range(np_):
-            w, b = omega[m : m + 1], bose[m : m + 1]
-            up, down = gap + w, gap - w
-            value = (b + fermi) * (scale / (up * up + SMEARING * SMEARING))
-            value += (b + 1.0 - fermi) * (scale / (down * down + SMEARING * SMEARING))
-            occ[m, :, at] = value
-    each(tiles, occupations, unroll=2)
 
     all_of(recvz, ni - 1, sems.at[9])
     terms = [own] + [recvz[chip(o)].astype(F32) for o in range(ni - 1)]
@@ -347,6 +331,31 @@
         return vrows.at[pl.ds(c * ni, ni)]
     give_v = copy(v_half(mc), v_half(mc), wsem.at[0], wsem.at[1], other)
     give_v.start()
+
+    copy(e_half(1 - mc), e_half(1 - mc), wsem.at[2], wsem.at[3], other).wait_recv()
+
+    lane1 = iota((1, LANES), 1) // NB
+    row_e = iota((rows, LANES), 0) % nb + mp * nb
+    e_col = jnp.sum(
+        jnp.where(iota((rows, LANES), 1) == row_e, esend[...], 0.0), axis=1, keepdims=True)
+
+    def occupations(t):
+        at = pl.ds(pl.multiple_of(t * LANES, LANES), LANES)
+        e4 = [egot[slots[1, 4 * t + g]] for g in range(4)]
+        e_there = jnp.where(lane1 < 2, jnp.where(lane1 == 0, e4[0], e4[1]), jnp.where(lane1 == 2, e4[2], e4[3]))
+        fermi = 1.0 / (1.0 + jnp.exp(e_there * (1.0 / THERMAL)))
+        gap = e_col - e_there
+        omega = phx[64 : 64 + np_, at]
+        bose = 1.0 / (jnp.exp(omega * (1.0 / THERMAL)) - 1.0)
+        scale = SMEARING / (math.pi * queries)
+        for m in range(np_):
+            w, b = omega[m : m + 1], bose[m : m + 1]
+            up, down = gap + w, gap - w
+            value = (b + fermi) * (scale / (up * up + SMEARING * SMEARING))
+            value += (b + 1.0 - fermi) * (scale / (down * down + SMEARING * SMEARING))
+            occ[m, :, at] = value
+    each(tiles, occupations, unroll=2)
+
 
     swap.wait_send()
     give_e.wait_send()

time: 33.5 us -> 31.5 us (0.940)
  Pallas kernels: 32.8 us -> 30.8 us
    pallas_call x1, Pallas kernels: 32.8 us -> 30.8 us  [shards(): pl.pallas_call(functools.partial(body, np_, ka, ql), out_shape=pltpu.VMEM...]
where the time goes in v5:
time: 31.5 us; the launch traced here: 31.3 us
  Pallas kernels  30.8 us (98%)
  local copies, waits for them, and re-layouts  0.51 us (2%)
    pallas_call x1, Pallas kernels, shards(): pl.pallas_call(functools.partial(body, np_, ka, ql), out_shape=pltpu.VMEM...  30.8 us

profile of v5, /device:TPU:1, one launch (start us, length us, event | category | flops | bytes accessed | tf_op | source)
XLA Modules:
  0.0 31.3 jit_solution(14070293267136248737)
XLA Ops:
  0.0 30.8 %self_energy.1 = f32[1,4]{1,0:T(1,128)S(1)} custom-call(bf16[320,2048]{1,0:T(8,128)(2,1)} %bitcast.6, f32[16,128]{1,0:T(8,128)} %bitcast.8, f32[1,32]{1,0:T(1,128)} %ener_in.1, s32[3,64]{1,0:T(4,128)} %kc_in.1, s32[3,320]{1,0:T(4,128)} %rc_in.1, s32[320]{0:T(512)} %deg_in.1, s32[1,12]{1,0:T(1,128)} %kq_in.1, f32[8,12]{1,0:T(8,128)} %bitcast.9, f32[64,12]{1,0:T(8,128)} %bitcast.7), custom_call_target="tpu_custom_call" | custom-call | tf_op jit(solution)/shard_map/self_energy/pallas_call | solution.py:424
  30.8 0.5 %copy.11 = f32[1,4]{1,0:T(1,128)} copy(f32[1,4]{1,0:T(1,128)S(1)} %self_energy.1) | data formatting | bytes 32

commit v6 on v5

--- a/solution.py
+++ b/solution.py
@@ -69,8 +69,10 @@
         y = lax.rem(my + 1 - lax.rem(o, 2), 2)
         return z * 2 + y
 
-    def in_z_order(f):
+    def in_z_order(f, before={}):
         for z in range(nz):
+            if z in before:
+                before[z]()
             f(z * 2 + 1 - my)
 
             @pl.when(mz != z)
@@ -93,6 +95,8 @@
     pl.semaphore_signal(barrier, inc=1, device_id=other, device_id_type=MESH)
     each(np_ - 1, lambda o: pl.semaphore_signal(
         barrier, inc=1, device_id={"pb": mate(o)}, device_id_type=MESH))
+    each(np_ - 1, lambda o: pl.semaphore_signal(
+        barrier, inc=1, device_id={"pb": mate(o), **other}, device_id_type=MESH))
 
     loads = [pltpu.make_async_copy(src, dst, small_sem.at[n]) for n, (src, dst) in enumerate([
         (kc_in, kc), (rc_in, rc), (deg_in, deg), (vec_in, vec), (ener_in, ener), (kq_in, kq), (om_in, om), (ph_in, ph)])]
@@ -168,7 +172,7 @@
     kqsend[...] = jnp.zeros_like(kqsend)
     kqsend[0:1, 0:ql] = kq[...]
 
-    pl.semaphore_wait(barrier, ni + np_ - 1)
+    pl.semaphore_wait(barrier, ni + 2 * (np_ - 1))
 
     def copy(src, dst, s, r, to):
         return pltpu.make_async_remote_copy(
@@ -178,8 +182,12 @@
         part = ref.at[pl.ds(0, count)]
         pltpu.make_async_copy(part, part, sem).wait()
 
-    swap = copy(sendc, recvc, csem.at[0], csem.at[1], other)
+    cut_at = 8
+    swap = copy(sendc.at[pl.ds(0, cut_at)], recvc.at[pl.ds(0, cut_at)], csem.at[0], csem.at[1], other)
+    swap_rest = copy(
+        sendc.at[pl.ds(cut_at, ni - cut_at)], recvc.at[pl.ds(cut_at, ni - cut_at)], wsem.at[0], wsem.at[1], other)
     swap.start()
+    swap_rest.start()
 
     def po_copy(o, to):
         return copy(posend, pogot.at[mp], sems.at[0], sems.at[1], {"pb": to})
@@ -226,7 +234,7 @@
     def add_and_send(i):
         sendz[i] = (of_point(2 * i + mc) + recvc[i].astype(F32)).astype(BF)
         z_copy(0, i).start()
-    in_z_order(add_and_send)
+    in_z_order(add_and_send, {cut_at // 2: swap_rest.wait_recv})
     own = of_point(me) + recvc[mi].astype(F32)
 
     for blk, (s0, c0, s1, c1) in enumerate(
@@ -281,7 +289,15 @@
 
     def vp_copy(o, p, to):
         return copy(v_block(p, mc), v_block(p, mc), sems.at[10], sems.at[11], {"pb": to})
-    each(np_ - 1, lambda o: vp_copy(o, mp, mate(o)).start())
+
+    def to_other_core(to):
+        return copy(v_block(mp, mc), v_block(mp, mc), sems.at[10], sems.at[11], {**to, **other})
+
+    def spread_v(o):
+        vp_copy(o, mp, mate(o)).start()
+        to_other_core({"pb": mate(o)}).start()
+    each(np_ - 1, spread_v)
+    to_other_core({}).start()
 
     for q in range(queries):
         point = kqs[q // ql, 0, q % ql]
@@ -325,13 +341,6 @@
     each(np_ - 1, lambda o: f_copy(o, mate(o)).start())
     fgot[mp] = fsend[mp]
 
-    all_of(vrows, (np_ - 1) * nj, sems.at[11])
-
-    def v_half(c):
-        return vrows.at[pl.ds(c * ni, ni)]
-    give_v = copy(v_half(mc), v_half(mc), wsem.at[0], wsem.at[1], other)
-    give_v.start()
-
     copy(e_half(1 - mc), e_half(1 - mc), wsem.at[2], wsem.at[3], other).wait_recv()
 
     lane1 = iota((1, LANES), 1) // NB
@@ -357,7 +366,10 @@
     each(tiles, occupations, unroll=2)
 
 
+    all_of(vrows, (2 * np_ - 1) * nj, sems.at[11])
+
     swap.wait_send()
+    swap_rest.wait_send()
     give_e.wait_send()
 
     all_of(sendz, ni - 1, sems.at[8])
@@ -372,9 +384,7 @@
         all_of(vrows, nj - 1, sems.at[6])
     all_of(pogot, np_ - 1, sems.at[0])
     all_of(kqgot, np_ - 1, sems.at[2])
-    all_of(vrows, (np_ - 1) * nj, sems.at[10])
-
-    copy(v_half(1 - mc), v_half(1 - mc), wsem.at[0], wsem.at[1], other).wait_recv()
+    all_of(vrows, (2 * np_ - 1) * nj, sems.at[10])
 
     def take(t):
         for g in range(4):
@@ -405,7 +415,6 @@
         jnp.where(iota((rows, LANES), 1) == iota((rows, LANES), 0) % nb, summed, 0.0),
         axis=0, keepdims=True)[:, :nb]
 
-    give_v.wait_send()
     all_of(fgot, np_ - 1, sems.at[12])
 
 

time: 31.5 us -> 31.4 us (level)
  no operation moved by 1% of the time
where the time goes in v6:
time: 31.4 us; the launch traced here: 31 us
  Pallas kernels  30.5 us (97%)
  local copies, waits for them, and re-layouts  0.51 us (2%)
    pallas_call x1, Pallas kernels, shards(): pl.pallas_call(functools.partial(body, np_, ka, ql), out_shape=pltpu.VMEM...  30.5 us

profile of v6, /device:TPU:1, one launch (start us, length us, event | category | flops | bytes accessed | tf_op | source)
XLA Modules:
  0.0 31.0 jit_solution(696744055324447865)
XLA Ops:
  0.0 30.5 %self_energy.1 = f32[1,4]{1,0:T(1,128)S(1)} custom-call(bf16[320,2048]{1,0:T(8,128)(2,1)} %bitcast.6, f32[16,128]{1,0:T(8,128)} %bitcast.8, f32[1,32]{1,0:T(1,128)} %ener_in.1, s32[3,64]{1,0:T(4,128)} %kc_in.1, s32[3,320]{1,0:T(4,128)} %rc_in.1, s32[320]{0:T(512)} %deg_in.1, s32[1,12]{1,0:T(1,128)} %kq_in.1, f32[8,12]{1,0:T(8,128)} %bitcast.9, f32[64,12]{1,0:T(8,128)} %bitcast.7), custom_call_target="tpu_custom_call" | custom-call | tf_op jit(solution)/shard_map/self_energy/pallas_call | solution.py:433
  30.5 0.5 %copy.11 = f32[1,4]{1,0:T(1,128)} copy(f32[1,4]{1,0:T(1,128)S(1)} %self_energy.1) | data formatting | bytes 32

commit v7 on v5

--- a/solution.py
+++ b/solution.py
@@ -43,8 +43,8 @@
     vec, ener, kc, rc, deg, kq, om, ph,
     xbuf, sums, sendc, recvc, sendz, recvz, vsend, vrows, esend, egot,
     flat, posend, pogot, kqsend, kqgot, kqs, spread, phx, fold, fsend, fgot,
-    slots, shifts, raw, vq, occ, small_sem,
-    xsem, csem, wsem, ksm, sems,
+    slots, shifts, raw, vq, occ,
+    csem, wsem, sems,
 ):
     ni = ka // 2
     nz = ni // 2
@@ -94,11 +94,11 @@
     each(np_ - 1, lambda o: pl.semaphore_signal(
         barrier, inc=1, device_id={"pb": mate(o)}, device_id_type=MESH))
 
-    loads = [pltpu.make_async_copy(src, dst, small_sem.at[n]) for n, (src, dst) in enumerate([
+    loads = [pltpu.make_async_copy(src, dst, (sems.at[2 * n] if n < 7 else csem.at[0])) for n, (src, dst) in enumerate([
         (kc_in, kc), (rc_in, rc), (deg_in, deg), (vec_in, vec), (ener_in, ener), (kq_in, kq), (om_in, om), (ph_in, ph)])]
     for c in loads[:3]:
         c.start()
-    load = pltpu.make_async_copy(coup, xbuf, xsem)
+    load = pltpu.make_async_copy(coup, xbuf, wsem.at[0])
     load.start()
     for c in loads[3:]:
         c.start()
@@ -253,7 +253,7 @@
 
     all_of(pogot, np_ - 1, sems.at[1])
     all_of(kqgot, np_ - 1, sems.at[3])
-    to_scalar = pltpu.make_async_copy(kqgot, kqs, ksm)
+    to_scalar = pltpu.make_async_copy(kqgot, kqs, wsem.at[0])
     to_scalar.start()
     got = pogot[...].reshape(np_ * SLOTS, LANES)
     if np_ * SLOTS < LANES:
@@ -461,8 +461,7 @@
             V((width // 8, 512), BF),
             V((64, width), BF),
             V((np_, rows, width), F32),
-            sem((8,)),
-            sem, sem((2,)), sem((4,)), sem, sem((14,)),
+            sem((2,)), sem((4,)), sem((14,)),
         ],
         compiler_params=pltpu.CompilerParams(collective_id=0, has_side_effects=True),
         name="self_energy",

time: 31.5 us -> 31.4 us (level)
  no operation moved by 1% of the time
where the time goes in v7:
time: 31.4 us; the launch traced here: 31.2 us
  Pallas kernels  30.7 us (98%)
  local copies, waits for them, and re-layouts  0.51 us (2%)
    pallas_call x1, Pallas kernels, shards(): pl.pallas_call(functools.partial(body, np_, ka, ql), out_shape=pltpu.VMEM...  30.7 us

profile of v7, /device:TPU:1, one launch (start us, length us, event | category | flops | bytes accessed | tf_op | source)
XLA Modules:
  0.0 31.2 jit_solution(7542882952529143173)
XLA Ops:
  0.0 30.7 %self_energy.1 = f32[1,4]{1,0:T(1,128)S(1)} custom-call(bf16[320,2048]{1,0:T(8,128)(2,1)} %bitcast.6, f32[16,128]{1,0:T(8,128)} %bitcast.8, f32[1,32]{1,0:T(1,128)} %ener_in.1, s32[3,64]{1,0:T(4,128)} %kc_in.1, s32[3,320]{1,0:T(4,128)} %rc_in.1, s32[320]{0:T(512)} %deg_in.1, s32[1,12]{1,0:T(1,128)} %kq_in.1, f32[8,12]{1,0:T(8,128)} %bitcast.9, f32[64,12]{1,0:T(8,128)} %bitcast.7), custom_call_target="tpu_custom_call" | custom-call | tf_op jit(solution)/shard_map/self_energy/pallas_call | solution.py:424
  30.7 0.5 %copy.11 = f32[1,4]{1,0:T(1,128)} copy(f32[1,4]{1,0:T(1,128)S(1)} %self_energy.1) | data formatting | bytes 32
